TPU v7x, 32 devices: a whole 2x2x4 slice. The times are simulated.
32 devices in a mesh: ctx: 8 (over z, x), tp: 4 (over y, core).
Axes of the slice: x: 2, y: 2, z: 4, core: 2. Of those that a mesh axis runs over, the one named last changes fastest.
Arguments:
- queries: bfloat16 [4096, 2048], P('ctx', 'tp'), may hold values from -40 to 40
- keys: bfloat16 [4096, 2048], P('ctx', 'tp'), may hold values from -40 to 40
- values: bfloat16 [4096, 2048], P('ctx', 'tp'), may hold values from -6 to 6
- out_weight: bfloat16 [2048, 4096], P('tp'), may hold values from -0.1875 to 0.1875
- doc_lengths: int32 [16], replicated, may hold values from 1 to 2048, 4096 in all
- layout: int32 [16], replicated, may hold values from 0 to 15, each once
Outputs:
- mixed: bfloat16 [4096, 4096], P('ctx', 'tp')
- log_totals: float32 [16, 4096], P('tp', 'ctx')
Inputs may be any that keep to these rules, and one draw needn't show every extreme that they name: `layout`: every block number appears once. `doc_lengths`: the lengths sum to 4096; the longest is exactly 2048.
All inputs are finite; a program needn't handle non-finite values.
Results may differ from a plain program's by a relative error of at most 0.012.
Values may be sent and summed in bfloat16 or wider, within the bound.
No kernel may reach another device: no remote copies, remote signals or barrier semaphores. Data moves between devices by JAX's collectives and lax.ppermute only.
A program may use at most 192 MiB of HBM per device.

v0:
```python
import math

import jax
import jax.numpy as jnp
from jax import lax
from jax.sharding import PartitionSpec as P

HEAD_DIM = 128


def positions_of(layout, first_row, count, half):
    rows = first_row + jnp.arange(count, dtype=jnp.int32)
    block_ids = rows // half
    table = jnp.arange(layout.shape[0], dtype=jnp.int32)
    owner = jnp.sum(jnp.where(block_ids[:, None] == table[None, :], layout[None, :], 0), axis=1)
    return owner * half + rows % half


def documents_of(starts, position):
    return jnp.sum((starts[None, :] <= position[:, None]).astype(jnp.int32), axis=1) - 1


def local(queries, keys, values, out_weight, doc_lengths, layout):
    rows = queries.shape[0]
    half = rows // 2
    heads = queries.shape[1] // HEAD_DIM
    scale = 1.0 / math.sqrt(HEAD_DIM)
    starts = jnp.cumsum(doc_lengths) - doc_lengths
    query_pos = positions_of(layout, lax.axis_index("ctx") * rows, rows, half)
    query_doc = documents_of(starts, query_pos)
    query_heads = queries.reshape(rows, heads, HEAD_DIM)

    def update(carry, key_blk, value_blk, allowed):
        top, totals, summed = carry
        scores = (
            jnp.einsum("qhd,khd->hqk", query_heads, key_blk, preferred_element_type=jnp.float32)
            * scale
        )
        scores = jnp.where(allowed[None], scores, -1e30)
        new_top = jnp.maximum(top, jnp.max(scores, axis=-1))
        weights = jnp.where(allowed[None], jnp.exp(scores - new_top[..., None]), 0.0)
        factor = jnp.exp(top - new_top)
        totals = totals * factor + jnp.sum(weights, axis=-1)
        summed = summed * factor.T[:, :, None] + jnp.einsum(
            "hqk,khd->qhd",
            weights.astype(jnp.bfloat16),
            value_blk,
            preferred_element_type=jnp.float32,
        )
        return (new_top, totals, summed)

    def tile(state, key_blk, value_blk, key_pos):
        key_doc = documents_of(starts, key_pos)
        allowed = (key_doc[None, :] == query_doc[:, None]) & (
            key_pos[None, :] <= query_pos[:, None]
        )
        return lax.cond(
            jnp.any(allowed),
            lambda inner: update(inner, key_blk, value_blk, allowed),
            lambda inner: inner,
            state,
        )

    initial = (
        jnp.full((heads, rows), -1e30, jnp.float32),
        jnp.zeros((heads, rows), jnp.float32),
        jnp.zeros((rows, heads, HEAD_DIM), jnp.float32),
    )
    key_piece = lax.all_gather(keys, "ctx", axis=0, tiled=True)
    value_piece = lax.all_gather(values, "ctx", axis=0, tiled=True)
    count = key_piece.shape[0]
    width = math.gcd(count, 512)

    def one_step(index, state):
        first = index * width
        key_blk = lax.dynamic_slice_in_dim(key_piece, first, width, 0).reshape(
            width, heads, HEAD_DIM
        )
        value_blk = lax.dynamic_slice_in_dim(value_piece, first, width, 0).reshape(
            width, heads, HEAD_DIM
        )
        key_pos = positions_of(layout, first, width, half)
        return tile(state, key_blk, value_blk, key_pos)

    top, totals, summed = lax.fori_loop(0, count // width, one_step, initial)
    attended = (summed / totals.T[:, :, None]).reshape(rows, heads * HEAD_DIM).astype(jnp.bfloat16)
    log_totals = top + jnp.log(totals)
    partial_value = jnp.dot(attended, out_weight, preferred_element_type=jnp.float32)
    mixed = lax.psum_scatter(
        partial_value.astype(jnp.bfloat16), "tp", scatter_dimension=1, tiled=True
    )
    return (mixed, log_totals)


def solution(mesh):
    placed = (P("ctx", "tp"), P("ctx", "tp"), P("ctx", "tp"), P("tp", None), P(), P())
    return jax.shard_map(
        local,
        mesh=mesh,
        in_specs=placed,
        out_specs=(P("ctx", "tp"), P("tp", "ctx")),
        check_vma=False,
    )
```

profile of v0, /device:TPU:0, one launch (start us, length us, event | category | flops | bytes accessed | tf_op | source)
XLA Modules:
  0.0 269.6 jit_solution(391481774716480319)
XLA Ops:
  7.2 2.0 copy.23
  9.3 0.0 all-gather.5.cloned.1.call-start
  9.3 2.1 copy.25
  11.5 0.0 reduce-scatter.2.cloned.1.call-start
  11.5 0.7 copy.22
  12.3 0.1 reduce
  12.4 0.7 sub.45
  13.1 1.3 copy.24
  14.3 0.3 copy.26
  14.6 0.1 select_reduce_fusion.1
  14.7 0.1 convert_reduce_fusion.1
  14.8 73.2 %all-gather.3.cloned.1.call-done = bf16[4096,512]{0,1:T(8,128)(2,1)} async-done(((bf16[512,512]{0,1:T(8,128)(2,1)}), bf16[4096,512]{0,1:T(8,128)(2,1)}) %all-gather.3.cloned.1.call-update) | async-done | bytes 4194320 | tf_op jit(solution)/shard_map/all_gather | solution.py:69
  88.0 74.9 %all-gather.5.cloned.1.call-done = bf16[4096,512]{0,1:T(8,128)(2,1)} async-done(((bf16[512,512]{0,1:T(8,128)(2,1)}), bf16[4096,512]{0,1:T(8,128)(2,1)}) %all-gather.5.cloned.1.call-update) | async-done | bytes 4194320 | tf_op jit(solution)/shard_map/all_gather | solution.py:70
  162.9 0.1 broadcast_in_dim.115
  163.0 34.8 %while.20 = (s32[]{:T(128)}, f32[4,512]{1,0:T(4,128)S(1)}, f32[4,512]{1,0:T(4,128)S(1)}, f32[512,4,128]{2,0,1:T(8,128)S(1)}, s32[16]{0:T(128)S(1)}, /*index=5*/s...) while((s32[]{:T(128)}, f32[4,512]{1,0:T(4,128)S(1)}, ...), condition=%wide.region_11.12_spmd, body=%wide.region_3.11_spmd.sunk | while | flops 552145408 | bytes 19556788 | solution.py:85
  163.0 0.1 select_reduce_fusion.3
  163.1 0.1 convert_reduce_fusion.3
  163.2 0.9 fusion.33
  164.7 5.2 %conditional.2 = ((f32[4,512]{1,0:T(4,128)S(1)}, f32[4,512]{1,0:T(4,128)S(1)}, f32[512,4,128]{2,0,1:T(8,128)S(1)})) conditional(s32[]{:T(128)} %convert_element_type.57, (f32[4,512]{1,0:T(4,128)S(1)}, f32[4,512]{1,0:T(4,128)S(1)}, f32[512,4,128]{2,0,1:T(8,128)S(1)}) %tuple.70, (pred[512,512]{0,1:T(8,128)(4,1)S(1)}, s32[]{:T(128)}, ...), branch_computations={%region_7.7_spmd, %region_8.10_spmd} | conditional | flops 551032832 | bytes 19267654 | solution.py:57
  164.7 1.3 constant_dynamic-slice_fusion
  166.0 1.0 fusion
  167.0 1.8 fusion.9
  168.8 1.0 fusion.2
  169.9 0.1 select_reduce_fusion.3
  170.1 0.1 convert_reduce_fusion.3
  170.1 0.9 fusion.33
  171.6 5.2 %conditional.2 = ((f32[4,512]{1,0:T(4,128)S(1)}, f32[4,512]{1,0:T(4,128)S(1)}, f32[512,4,128]{2,0,1:T(8,128)S(1)})) conditional(s32[]{:T(128)} %convert_element_type.57, (f32[4,512]{1,0:T(4,128)S(1)}, f32[4,512]{1,0:T(4,128)S(1)}, f32[512,4,128]{2,0,1:T(8,128)S(1)}) %tuple.70, (pred[512,512]{0,1:T(8,128)(4,1)S(1)}, s32[]{:T(128)}, ...), branch_computations={%region_7.7_spmd, %region_8.10_spmd} | conditional | flops 551032832 | bytes 19267654 | solution.py:57
  171.7 1.3 constant_dynamic-slice_fusion
  172.9 1.0 fusion
  174.0 1.8 fusion.9
  175.8 1.0 fusion.2
  176.9 0.1 select_reduce_fusion.3
  177.0 0.1 convert_reduce_fusion.3
  177.1 0.9 fusion.33
  178.6 0.1 select_reduce_fusion.3
  178.7 0.1 convert_reduce_fusion.3
  178.8 0.9 fusion.33
  180.4 0.1 select_reduce_fusion.3
  180.5 0.1 convert_reduce_fusion.3
  180.6 0.9 fusion.33
  182.1 5.2 %conditional.2 = ((f32[4,512]{1,0:T(4,128)S(1)}, f32[4,512]{1,0:T(4,128)S(1)}, f32[512,4,128]{2,0,1:T(8,128)S(1)})) conditional(s32[]{:T(128)} %convert_element_type.57, (f32[4,512]{1,0:T(4,128)S(1)}, f32[4,512]{1,0:T(4,128)S(1)}, f32[512,4,128]{2,0,1:T(8,128)S(1)}) %tuple.70, (pred[512,512]{0,1:T(8,128)(4,1)S(1)}, s32[]{:T(128)}, ...), branch_computations={%region_7.7_spmd, %region_8.10_spmd} | conditional | flops 551032832 | bytes 19267654 | solution.py:57
  182.1 1.3 constant_dynamic-slice_fusion
  183.4 1.0 fusion
  184.4 1.8 fusion.9
  186.2 1.0 fusion.2
  187.3 0.1 select_reduce_fusion.3
  187.4 0.1 convert_reduce_fusion.3
  187.5 0.9 fusion.33
  189.1 0.1 select_reduce_fusion.3
  189.2 0.1 convert_reduce_fusion.3
  189.3 0.9 fusion.33
  190.8 5.2 %conditional.2 = ((f32[4,512]{1,0:T(4,128)S(1)}, f32[4,512]{1,0:T(4,128)S(1)}, f32[512,4,128]{2,0,1:T(8,128)S(1)})) conditional(s32[]{:T(128)} %convert_element_type.57, (f32[4,512]{1,0:T(4,128)S(1)}, f32[4,512]{1,0:T(4,128)S(1)}, f32[512,4,128]{2,0,1:T(8,128)S(1)}) %tuple.70, (pred[512,512]{0,1:T(8,128)(4,1)S(1)}, s32[]{:T(128)}, ...), branch_computations={%region_7.7_spmd, %region_8.10_spmd} | conditional | flops 551032832 | bytes 19267654 | solution.py:57
  190.8 1.3 constant_dynamic-slice_fusion
  192.1 1.0 fusion
  193.1 1.8 fusion.9
  194.9 1.0 fusion.2
  196.0 0.1 select_reduce_fusion.3
  196.1 0.1 convert_reduce_fusion.3
  196.2 0.9 fusion.33
  197.7 0.3 copy.27
  198.1 0.1 divide_convert_fusion
  198.2 6.5 %convolution_convert_fusion = bf16[512,4096]{1,0:T(8,128)(2,1)} fusion(bf16[512,512]{0,1:T(8,128)(2,1)S(1)} %bitcast.34, bf16[512,4096]{1,0:T(8,128)(2,1)} %param.13), kind=kOutput, calls=%fused_computation.33 | convolution fusion | flops 2149580800 | bytes 8912896 | tf_op jit(solution)/shard_map/dot_general | solution.py:88
  204.7 0.6 log_add_fusion
  205.3 57.7 %reduce-scatter.2.cloned.1.call-done = bf16[512,1024]{1,0:T(8,128)(2,1)} async-done(((bf16[512,4096]{1,0:T(8,128)(2,1)}), bf16[512,1024]{1,0:T(8,128)(2,1)}) %reduce-scatter.2.cloned.1.call-update) | async-done | bytes 1048592 | tf_op jit(solution)/shard_map/reduce_scatter | solution.py:89
  (52 shorter events, 0.6 us)
Async XLA Ops:
  7.2 7.5 %copy-start = (s32[16]{0:T(128)S(1)}, s32[16]{0:T(128)}, u32[]{:S(2)}) copy-start(s32[16]{0:T(128)} %param.15) | copy-start | bytes 196
  7.2 80.8 %all-gather.3.cloned.1.call-start = ((), (), s32[]{:S(2)}) async-start(), calls=%async_computation.1 | async-start | bytes 4718592 | tf_op jit(solution)/shard_map/all_gather | solution.py:69
  9.3 153.6 %all-gather.5.cloned.1.call-start = ((), (), s32[]{:S(2)}) async-start(), calls=%async_computation.2 | async-start | bytes 4718592 | tf_op jit(solution)/shard_map/all_gather | solution.py:70
  11.5 251.6 %reduce-scatter.2.cloned.1.call-start = ((), (), s32[]{:S(2)}) async-start(), calls=%async_computation.3 | async-start | bytes 5242880 | tf_op jit(solution)/shard_map/reduce_scatter | solution.py:89
Sparse Core Ops, SparseCore 0:
  10.6 77.3 all-gather.2
  90.0 72.8 all-gather.4
  204.9 58.1 reduce-scatter.1
where the time goes:
time: 267 us; the launch traced here: 270 us
  waiting for transfers between devices  206 us (77%)
  matrix products  17.7 us (7%)
  other arithmetic  15 us (6%)
  between operations  13.8 us (5%)
  local copies, waits for them, and re-layouts  11.9 us (4%)
  loops' own time  5.17 us (2%)
    all_gather x1, waiting for transfers between devices, local(): value_piece = lax.all_gather(values, 'ctx', axis=0, tiled=True)  74.9 us
    all_gather x1, waiting for transfers between devices, local(): key_piece = lax.all_gather(keys, 'ctx', axis=0, tiled=True)  73.2 us
    reduce_scatter x1, waiting for transfers between devices, local(): lax.psum_scatter(partial_value.astype(jnp.bfloat16), 'tp', scatter_dimens...  57.7 us
    reduce_or x8, other arithmetic, tile(): jnp.any(allowed)  7.31 us
    dot_general x4, matrix products, update(): jnp.einsum('hqk,khd->qhd', weights.astype(jnp.bfloat16), value_blk, prefe...  7.14 us
    dot_general x1, matrix products, local(): jnp.dot(attended, out_weight, preferred_element_type=jnp.float32)  6.49 us
    unnamed x5, local copies, waits for them, and re-layouts  5.4 us
  transfers between devices with their start and end apart: 3, of which 3 were waited for; matrix products, arithmetic and copies ran while one was open for 2% of the time, Pallas kernels for 0%

commit v1 on v0

v1 whole, which is shorter than its diff:
```python
import functools
import math

import jax
import jax.numpy as jnp
from jax import lax
from jax.experimental import pallas as pl
from jax.experimental.pallas import tpu as pltpu
from jax.sharding import PartitionSpec as P

HEAD_DIM = 128
NEG = -1e30
LOG_ROWS = 16
ONES = 16
LONE, LAST = 3, 2
PACK_ORDER = (3, 1, 0, 2)
ATTEND_ORDER = (3, 1, 2, 0)


HBM_SPEC = pl.BlockSpec(memory_space=pltpu.MemorySpace.HBM)
VMEM_SPEC = pl.BlockSpec(memory_space=pltpu.MemorySpace.VMEM)
MIB = 1 << 20
SMEM_SPEC = pl.BlockSpec(memory_space=pltpu.MemorySpace.SMEM)


def pack_kernel(places, spread, k_ref, v_ref, q_ref, *refs):
    kv_out, q_out, (v_rows, sems) = refs[:places], refs[places : 2 * places], refs[2 * places :]
    z = lax.axis_index("ctx") // spread
    rows = k_ref.shape[0]
    copies = []
    for s in PACK_ORDER:
        columns = pl.ds(pl.multiple_of((z ^ s) * HEAD_DIM, HEAD_DIM), HEAD_DIM)
        copies.append(
            [
                pltpu.make_async_copy(v_ref.at[:, columns], v_rows.at[s], sems.at[s, 0]),
                pltpu.make_async_copy(k_ref.at[:, columns], kv_out[s].at[0], sems.at[s, 1]),
                pltpu.make_async_copy(q_ref.at[:, columns], q_out[s], sems.at[s, 2]),
            ]
        )
    for group in copies:
        for copy in group:
            copy.start()
    for s, group in zip(PACK_ORDER, copies):
        group[0].wait()
        for i in range(0, rows, HEAD_DIM):
            kv_out[s][1, i : i + HEAD_DIM, :] = v_rows[s, i : i + HEAD_DIM, :].T
    for group in copies:
        group[1].wait()
        group[2].wait()


def pack(keys, values, queries, places, spread):
    rows = keys.shape[0]
    return pl.pallas_call(
        functools.partial(pack_kernel, places, spread),
        out_shape=[jax.ShapeDtypeStruct((2, rows, HEAD_DIM), keys.dtype)] * places
        + [jax.ShapeDtypeStruct((rows, HEAD_DIM), keys.dtype)] * places,
        in_specs=[HBM_SPEC] * 3,
        out_specs=[VMEM_SPEC] * (2 * places),
        scratch_shapes=[
            pltpu.VMEM((places, rows, HEAD_DIM), keys.dtype),
            pltpu.SemaphoreType.DMA((places, 3)),
        ],
        compiler_params=pltpu.CompilerParams(vmem_limit_bytes=8 * MIB),
        name="pack",
    )(*(pltpu.with_memory_space_constraint(x, pltpu.HBM) for x in (keys, values, queries)))


def plan_kernel(places, spread, half, layout_ref, lens_ref, table_ref, bounds_ref):
    me = lax.axis_index("ctx")
    z, r = me // spread, me % spread
    count = 2 * places
    blocks = [layout_ref[((z ^ (i // 2)) * spread + r) * 2 + i % 2] for i in range(count)]
    index = lax.broadcasted_iota(jnp.int32, (count, half), 0)
    row_pos = lax.broadcasted_iota(jnp.int32, (count, half), 1)
    for i, block in enumerate(blocks):
        row_pos = row_pos + jnp.where(index == i, block * half, 0)

    def scan(j, carry):
        end, row_start, *lows = carry
        lows = [jnp.where(end <= block * half, end, low) for block, low in zip(blocks, lows)]
        row_start = jnp.where(row_pos >= end, end, row_start)
        return end + lens_ref[j], row_start, *lows

    zero = jnp.int32(0)
    _, row_start, *lows = lax.fori_loop(
        0, lens_ref.shape[0], scan, (zero, jnp.zeros((count, half), jnp.int32), *([zero] * count))
    )
    for i in range(count):
        table_ref[2 * i] = blocks[i]
        table_ref[2 * i + 1] = lows[i] // half
    bounds_ref[:count, :] = row_start
    bounds_ref[count:, :] = row_pos - row_start


def plan(layout, doc_lengths, places, spread, half):
    return pl.pallas_call(
        functools.partial(plan_kernel, places, spread, half),
        out_shape=[
            jax.ShapeDtypeStruct((4 * places,), jnp.int32),
            jax.ShapeDtypeStruct((4 * places, half), jnp.int32),
        ],
        in_specs=[SMEM_SPEC] * 2,
        out_specs=[SMEM_SPEC, VMEM_SPEC],
        compiler_params=pltpu.CompilerParams(vmem_limit_bytes=2 * MIB),
        name="plan",
    )(layout, doc_lengths)


def pack_weight_kernel(tp, columns, w_ref, *refs):
    outs, sems = refs[:-1], refs[-1]
    me, side = lax.axis_index("tp"), lax.axis_index("ctx") % 2
    copies = []
    for m in range(tp):
        depth = outs[m].shape[0]
        first = 0 if depth == w_ref.shape[0] else pl.multiple_of(side * depth, depth)
        copies.append(
            pltpu.make_async_copy(
                w_ref.at[
                    pl.ds(first, depth), pl.ds(pl.multiple_of((me ^ m) * columns, columns), columns)
                ],
                outs[m],
                sems.at[m],
            )
        )
    for copy in copies:
        copy.start()
    for copy in copies:
        copy.wait()


def pack_weight(weight, tp):
    depth, columns = weight.shape[0], weight.shape[1] // tp
    return pl.pallas_call(
        functools.partial(pack_weight_kernel, tp, columns),
        out_shape=[
            jax.ShapeDtypeStruct((depth // (1 if m < tp - 1 else 2), columns), weight.dtype)
            for m in range(tp)
        ],
        in_specs=[HBM_SPEC],
        out_specs=[VMEM_SPEC] * tp,
        scratch_shapes=[pltpu.SemaphoreType.DMA((tp,))],
        compiler_params=pltpu.CompilerParams(vmem_limit_bytes=8 * MIB),
        name="pack_weight",
    )(pltpu.with_memory_space_constraint(weight, pltpu.HBM))


def attention_kernel(place, places, spread, layout_ref, table_ref, bounds_ref, q_ref, *refs):
    refs, (scores, peaks, tops, summed) = refs[:-4], refs[-4:]
    sort = len(refs) != 3
    if sort:
        kv_refs, (out_ref, k_all, v_all) = refs[:-3], refs[-3:]
    else:
        k_all, v_all, out_ref = refs
    rows = q_ref.shape[0]
    half = rows // 2
    width = 2 * half
    factor = math.log2(math.e) / math.sqrt(HEAD_DIM)

    if sort:
        me = lax.axis_index("ctx")
        z, r = me // spread, me % spread
        for s in range(places):
            for t in range(spread):
                owner = (z ^ s) * spread + (r + spread - t) % spread
                chunk = kv_refs[s * spread + t]
                for b in range(2):
                    first = pl.multiple_of(layout_ref[owner * 2 + b] * half, half)
                    k_all[pl.ds(first, half), :] = chunk[0, b * half : (b + 1) * half, :]
                    for i in range(0, half, HEAD_DIM):
                        columns = pl.ds(pl.multiple_of(first + i, HEAD_DIM), HEAD_DIM)
                        v_all[:HEAD_DIM, columns] = chunk[
                            1, b * half + i : b * half + i + HEAD_DIM, :
                        ]
        total = layout_ref.shape[0] * half
        k_all[total:, :] = jnp.zeros((half, HEAD_DIM), k_all.dtype)
        v_all[:HEAD_DIM, total:] = jnp.zeros((HEAD_DIM, half), v_all.dtype)
        v_all[HEAD_DIM:, :] = jnp.ones((ONES, total + half), v_all.dtype)

    blocks = [table_ref[4 * place + 2 * b] for b in range(2)]
    lows = [table_ref[4 * place + 2 * b + 1] for b in range(2)]
    counts = [(blocks[b] - lows[b] + 2) // 2 for b in range(2)]
    items = counts[0] + counts[1]
    key_row = lax.broadcasted_iota(jnp.int32, (width, half), 0)
    tops[...] = jnp.full(tops.shape, NEG, jnp.float32)
    summed[...] = jnp.zeros(summed.shape, jnp.float32)

    def where_of(item):
        late = jnp.logical_and(item >= counts[0], item < items).astype(jnp.int32)
        low = jnp.where(late == 1, lows[1], lows[0])
        step = jnp.where(item < items, item - late * counts[0], 0)
        base = pl.multiple_of((low + 2 * step) * half, half)
        return late, base

    def score(item, slot):
        late, base = where_of(item)
        raw = lax.dot_general(
            k_all[pl.ds(base, width), :],
            q_ref[pl.ds(pl.multiple_of(late * half, half), half), :],
            (((1,), (1,)), ((), ())),
            preferred_element_type=jnp.float32,
        )
        row = 2 * place + late
        start = bounds_ref[pl.ds(row, 1), :] - jnp.where(item < items, base, -(1 << 30))
        span = bounds_ref[pl.ds(2 * places + row, 1), :].astype(jnp.uint32)
        masked = jnp.where((key_row - start).astype(jnp.uint32) <= span, raw, NEG)
        scores[slot] = masked
        peaks[slot] = jnp.max(masked, axis=0, keepdims=True)

    def absorb(item, slot):
        late, base = where_of(item)
        top = tops[late]
        new_top = jnp.maximum(top, peaks[slot])
        weights = jnp.exp2((scores[slot] - new_top) * factor)
        scale = jnp.exp2((top - new_top) * factor)
        tops[late] = new_top
        summed[late] = summed[late] * scale + jnp.dot(
            v_all[:, pl.ds(base, width)],
            weights.astype(jnp.bfloat16),
            preferred_element_type=jnp.float32,
        )

    score(0, 0)

    def pair(i, carry):
        score(2 * i + 1, 1)
        absorb(2 * i, 0)
        score(2 * i + 2, 0)
        absorb(2 * i + 1, 1)
        return carry

    lax.fori_loop(0, (items + 1) // 2, pair, 0)

    log_rows = []
    for b in range(2):
        sums = summed[b, HEAD_DIM : HEAD_DIM + 1, :]
        mean = summed[b, :HEAD_DIM, :] / sums
        out_ref[b * half : (b + 1) * half, :] = mean.T.astype(jnp.bfloat16)
        logs = tops[b] * (1.0 / math.sqrt(HEAD_DIM)) + jnp.log(sums)
        log_rows += [logs[:, i : i + HEAD_DIM] for i in range(0, half, HEAD_DIM)]
    left = jnp.concatenate(log_rows, axis=0)
    split = []
    for _ in range(3):
        piece = left.astype(jnp.bfloat16).astype(jnp.float32)
        split.append(piece)
        left = left - piece
    split.append(jnp.zeros((LOG_ROWS - 3 * len(log_rows), HEAD_DIM), jnp.float32))
    out_ref[pl.ds(rows, LOG_ROWS), :] = jnp.concatenate(split, axis=0).astype(jnp.bfloat16)


def attend(layout, table, bounds, query, sources, place, places, spread):
    rows = query.shape[0]
    half = rows // 2
    total = layout.shape[0] * half
    first = len(sources) != 2
    out_shape = [jax.ShapeDtypeStruct((rows + LOG_ROWS, HEAD_DIM), jnp.bfloat16)]
    if first:
        out_shape += [
            jax.ShapeDtypeStruct((total + half, HEAD_DIM), jnp.bfloat16),
            jax.ShapeDtypeStruct((HEAD_DIM + ONES, total + half), jnp.bfloat16),
        ]
    return pl.pallas_call(
        functools.partial(attention_kernel, place, places, spread),
        out_shape=out_shape,
        in_specs=[SMEM_SPEC] * 2 + [VMEM_SPEC] * (2 + len(sources)),
        out_specs=[VMEM_SPEC] * len(out_shape),
        scratch_shapes=[
            pltpu.VMEM((2, 2 * half, half), jnp.float32),
            pltpu.VMEM((2, 1, half), jnp.float32),
            pltpu.VMEM((2, 1, half), jnp.float32),
            pltpu.VMEM((2, HEAD_DIM + ONES, half), jnp.float32),
        ],
        compiler_params=pltpu.CompilerParams(vmem_limit_bytes=24 * MIB),
    )(layout, table, bounds, query, *sources)


def weight_rows(w_refs, m, z, side, s, pair):
    head = z ^ s
    count = 2 * HEAD_DIM if pair else HEAD_DIM
    if m < len(w_refs) - 2:
        first = (head // 2) * 2 if pair else head
        return w_refs[m][pl.ds(pl.multiple_of(first * HEAD_DIM, count), count), :]
    rows = pl.ds(0 if pair else pl.multiple_of((head % 2) * HEAD_DIM, HEAD_DIM), count)
    near, far = w_refs[-2:]
    return jnp.where(head // 2 == side, near[rows, :], far[rows, :])


def lone_terms(parts, w_refs, tp, z, side, s):
    total = None
    for m in range(0, tp, 2):
        left = jnp.concatenate([parts[m], parts[m + 1]], axis=1)
        right = jnp.concatenate(
            [weight_rows(w_refs, m + i, z, side, s, False) for i in range(2)], axis=0
        )
        term = jnp.dot(left, right, preferred_element_type=jnp.float32)
        total = term if total is None else total + term
    return total


def early_kernel(spread, tp, *refs):
    parts, w_refs, out_ref = refs[: 3 * tp], refs[3 * tp : -1], refs[-1]
    rows = out_ref.shape[0]
    me = lax.axis_index("ctx")
    z, side = me // spread, me % 2
    total = lone_terms([parts[2 * tp + m][:rows, :] for m in range(tp)], w_refs, tp, z, side, LONE)
    turn = z % 2 == 1
    for m in range(tp):
        here, there = parts[m][:rows, :], parts[tp + m][:rows, :]
        left = jnp.concatenate(
            [jnp.where(turn, there, here), jnp.where(turn, here, there)], axis=1
        )
        right = weight_rows(w_refs, m, z, side, 0, True)
        total = total + jnp.dot(left, right, preferred_element_type=jnp.float32)
    out_ref[...] = total


def late_kernel(places, spread, tp, *refs):
    parts, logs_in, w_refs = refs[:tp], refs[tp : tp + places - 1], refs[tp + places - 1 : -3]
    early_ref, out_ref, log_ref = refs[-3:]
    rows = out_ref.shape[0]
    me = lax.axis_index("ctx")
    z, side = me // spread, me % 2
    term = lone_terms([part[:rows, :] for part in parts], w_refs, tp, z, side, LAST)
    out_ref[...] = (early_ref[...] + term).astype(out_ref.dtype)
    count = rows // HEAD_DIM
    logs = {}
    for s, part in zip((0, 1, LONE, LAST), (*logs_in, parts[0])):
        tail = part[pl.ds(rows, LOG_ROWS), :].astype(jnp.float32)
        logs[s] = tail[:count] + tail[count : 2 * count] + tail[2 * count : 3 * count]
    for head in range(places):
        mine = logs[0]
        for s in range(1, places):
            mine = jnp.where(z ^ s == head, logs[s], mine)
        for i in range(count):
            log_ref[head : head + 1, i * HEAD_DIM : (i + 1) * HEAD_DIM] = mine[i : i + 1, :]


def project(groups, weights, places, spread, tp):
    rows = groups[0][0].shape[0] - LOG_ROWS
    columns = weights[0].shape[1]
    params = pltpu.CompilerParams(vmem_limit_bytes=16 * MIB)
    early_parts = [groups[m][s] for s in (0, 1, LONE) for m in range(tp)]
    early = pl.pallas_call(
        functools.partial(early_kernel, spread, tp),
        out_shape=jax.ShapeDtypeStruct((rows, columns), jnp.float32),
        in_specs=[VMEM_SPEC] * (len(early_parts) + len(weights)),
        out_specs=VMEM_SPEC,
        compiler_params=params,
        name="early",
    )(*early_parts, *weights)
    late_parts = [groups[m][LAST] for m in range(tp)] + [groups[0][s] for s in (0, 1, LONE)]
    return pl.pallas_call(
        functools.partial(late_kernel, places, spread, tp),
        out_shape=[
            jax.ShapeDtypeStruct((rows, columns), jnp.bfloat16),
            jax.ShapeDtypeStruct((places, rows), jnp.float32),
        ],
        in_specs=[VMEM_SPEC] * (len(late_parts) + len(weights) + 1),
        out_specs=[VMEM_SPEC] * 2,
        compiler_params=params,
        name="late",
    )(*late_parts, *weights, early)


def local(ctx, tp, queries, keys, values, out_weight, doc_lengths, layout):
    places = queries.shape[1] // HEAD_DIM
    spread = ctx // places
    assert places == 4 and tp == 4 and spread % 2 == 0

    def move(array, axis, target):
        count = ctx if axis == "ctx" else tp
        return lax.ppermute(array, axis, [(i, target(i)) for i in range(count)])

    def over_places(array, s):
        return move(array, "ctx", lambda i: ((i // spread) ^ s) * spread + i % spread)

    def over_spread(array, t):
        return move(array, "ctx", lambda i: i // spread * spread + (i % spread + t) % spread)

    def over_tp(array, m):
        return move(array, "tp", lambda i: i ^ m)

    packed = pack(keys, values, queries, places, spread)
    kv, q = packed[:places], packed[places:]
    q = [q[0]] + [over_places(q[s], s) for s in range(1, places)]
    sources = []
    for s in range(places):
        sources.append(over_places(kv[s], s) if s else kv[0])
        sources += [over_spread(sources[-1], t) for t in range(1, spread)]

    packed_weight = pack_weight(out_weight, tp)
    weights = [packed_weight[0]] + [over_tp(packed_weight[m], m) for m in range(1, tp)]
    weights.append(move(weights[-1], "ctx", lambda i: i ^ 1))

    table, bounds = plan(layout, doc_lengths, places, spread, keys.shape[0] // 2)
    heads = [None] * places
    for s in ATTEND_ORDER:
        message, *rest = attend(layout, table, bounds, q[s], sources, s, places, spread)
        sources = rest or sources
        heads[s] = over_places(message, s) if s else message

    groups = [heads]
    groups.append([over_tp(heads[s], 1) for s in range(places)])
    groups.append([over_tp(heads[s], 2) for s in range(places)])
    groups.append([over_tp(groups[2][s], 1) for s in range(places)])
    return project(groups, weights, places, spread, tp)


def solution(mesh):
    placed = (P("ctx", "tp"), P("ctx", "tp"), P("ctx", "tp"), P("tp", None), P(), P())
    return jax.shard_map(
        functools.partial(local, mesh.shape["ctx"], mesh.shape["tp"]),
        mesh=mesh,
        in_specs=placed,
        out_specs=(P("ctx", "tp"), P("tp", "ctx")),
        check_vma=False,
    )
```

time: 267 us -> 105 us (0.39)
  waiting for transfers between devices: 206 us -> 39.4 us
  starting transfers between devices: 0.12 us -> 48.8 us
  matrix products: 17.7 us -> 0 us
  Pallas kernels: 0 us -> 16 us
  other arithmetic: 15 us -> 0 us
  between operations: 13.8 us -> 0.75 us
  local copies, waits for them, and re-layouts: 11.9 us -> 0.01 us
  loops' own time: 5.17 us -> 0 us
    all_gather x2 -> x0, waiting for transfers between devices: 148 us -> none  [the longest x1 74.9 us: local(): value_piece = lax.all_gather(values, 'ctx', axis=0, tiled=True)]
    reduce_scatter x1 -> x0, waiting for transfers between devices: 57.7 us -> none  [local(): lax.psum_scatter(partial_value.astype(jnp.bfloat16), 'tp', scatter_dimens...]
    ppermute x0 -> x29, starting transfers between devices: none -> 48.8 us  [move(): return lax.ppermute(array, axis, [(i, target(i)) for i in range(count)])]
    ppermute x0 -> x29, waiting for transfers between devices: none -> 39.4 us  [move(): return lax.ppermute(array, axis, [(i, target(i)) for i in range(count)])]
    dot_general x9 -> x0, matrix products: 17.7 us -> none  [the longest x4 7.14 us: update(): jnp.einsum('hqk,khd->qhd', weights.astype(jnp.bfloat16), value_blk, prefe...]
    pallas_call x0 -> x9, Pallas kernels: none -> 16 us  [the longest x4 7.38 us: attend(): pl.pallas_call(functools.partial(attention_kernel, place, places, spread)...]
    reduce_or x8 -> x0, other arithmetic: 7.31 us -> none  [tile(): jnp.any(allowed)]
    reduce_sum x22 -> x0, other arithmetic: 5.77 us -> none  [the longest x4 4.16 us: update(): totals = totals * factor + jnp.sum(weights, axis=-1)]
  transfers between devices with their start and end apart: 3 -> 29, of which waited for: 3 -> 12; matrix products, arithmetic and copies ran while one was open for 2% -> 0% of each run, Pallas kernels for 0% -> 12%
where the time goes in v1:
time: 105 us
  starting transfers between devices  48.8 us (46%)
  waiting for transfers between devices  39.4 us (38%)
  Pallas kernels  16 us (15%)
    ppermute x29, starting transfers between devices, move(): return lax.ppermute(array, axis, [(i, target(i)) for i in range(count)])  48.8 us
    ppermute x29, waiting for transfers between devices, move(): return lax.ppermute(array, axis, [(i, target(i)) for i in range(count)])  39.4 us
    pallas_call x4, Pallas kernels, attend(): pl.pallas_call(functools.partial(attention_kernel, place, places, spread)...  7.38 us
  transfers between devices with their start and end apart: 29, of which 12 were waited for; matrix products, arithmetic and copies ran while one was open for 0% of the time, Pallas kernels for 12%

profile of v1, /device:TPU:0, one launch (start us, length us, event | category | flops | bytes accessed | tf_op | source)
XLA Modules:
  0.0 105.0 jit_solution(6938880801608634389)
XLA Ops:
  0.6 1.6 %pack.1 = (bf16[2,512,128]{2,1,0:T(8,128)(2,1)S(1)}, bf16[2,512,128]{2,1,0:T(8,128)(2,1)S(1)}, bf16[2,512,128]{2,1,0:T(8,128)(2,1)S(1)}, bf16[2,512,128]{2,1,0:T...) custom-call(bf16[512,512]{1,0:T(8,128)(2,1)} %k_ref.1, ...), custom_call_target="tpu_custom_call" | custom-call | tf_op jit(solution)/shard_map/pack/pallas_call | solution.py:54
  2.3 3.1 %collective-permute-start.3 = (bf16[2,512,128]{2,1,0:T(8,128)(2,1)S(1)}, bf16[2,512,128]{2,1,0:T(8,128)(2,1)S(1)}, u32[]{:S(2)}, u32[]{:S(2)}) collective-permute-start(bf16[2,512,128]{2,1,0:T(8,128)(2,1)S(1)} %get-tuple-element.24), channel_id=1, source_target_pairs={{0,8},{4,12},{8,0},{12,4},{16,24},{20,28},{24,16},{28,20},{1,9},{5... | collective-permute-start | bytes 786440 | tf_op jit(solution)/shard_map/ppermute | solution.py:372
  5.4 2.6 %collective-permute-start.5 = (bf16[2,512,128]{2,1,0:T(8,128)(2,1)S(1)}, bf16[2,512,128]{2,1,0:T(8,128)(2,1)S(1)}, u32[]{:S(2)}, u32[]{:S(2)}) collective-permute-start(bf16[2,512,128]{2,1,0:T(8,128)(2,1)S(1)} %get-tuple-element.25), channel_id=1, source_target_pairs={{0,16},{4,20},{8,24},{12,28},{16,0},{20,4},{24,8},{28,12},{1,17},{... | collective-permute-start | bytes 786440 | tf_op jit(solution)/shard_map/ppermute | solution.py:372
  8.0 0.0 collective-permute-start.7
  8.0 3.8 %collective-permute-start.1 = (bf16[512,128]{1,0:T(8,128)(2,1)S(1)}, bf16[512,128]{1,0:T(8,128)(2,1)S(1)}, u32[]{:S(2)}, u32[]{:S(2)}) collective-permute-start(bf16[512,128]{1,0:T(8,128)(2,1)S(1)} %get-tuple-element.22), channel_id=1, source_target_pairs={{0,24},{4,28},{8,16},{12,20},{16,8},{20,12},{24,0},{28,4},{1,25},{... | collective-permute-start | bytes 393224 | tf_op jit(solution)/shard_map/ppermute | solution.py:372
  11.8 2.0 %pack_weight.1 = (bf16[512,1024]{1,0:T(8,128)(2,1)S(1)}, bf16[512,1024]{1,0:T(8,128)(2,1)S(1)}, bf16[512,1024]{1,0:T(8,128)(2,1)S(1)}, bf16[256,1024]{1,0:T(8,128)(2,1)S(1)}) custom-call(bf16[512,4096]{1,0:T(8,128)(2,1)} %w_ref.1), custom_call_target="tpu_custom_call" | custom-call | tf_op jit(solution)/shard_map/pack_weight/pallas_call | solution.py:134
  13.8 0.1 collective-permute-start.18
  13.9 14.1 %collective-permute-done.1.q_ref = bf16[512,128]{1,0:T(8,128)(2,1)S(1)} collective-permute-done((bf16[512,128]{1,0:T(8,128)(2,1)S(1)}, bf16[512,128]{1,0:T(8,128)(2,1)S(1)}, u32[]{:S(2)}, u32[]{:S(2)}) %collective-permute-start.1) | collective-permute-done | bytes 131104 | tf_op jit(solution)/shard_map/ppermute | solution.py:372
  28.0 1.5 %collective-permute-start.2 = (bf16[2,512,128]{2,1,0:T(8,128)(2,1)S(1)}, bf16[2,512,128]{2,1,0:T(8,128)(2,1)S(1)}, u32[]{:S(2)}, u32[]{:S(2)}) collective-permute-start(bf16[2,512,128]{2,1,0:T(8,128)(2,1)S(1)} %get-tuple-element.23.refs_0_), channel_id=1, source_target_pairs={{0,4},{4,0},{8,12},{12,8},{16,20},{20,16},{24,28},{28,24},{1,5},{5... | collective-permute-start | bytes 786440 | tf_op jit(solution)/shard_map/ppermute | solution.py:372
  29.5 0.0 collective-permute-done.3.refs_2_
  29.5 0.5 collective-permute-start.4
  30.1 0.0 collective-permute-done.5.refs_4_
  30.1 1.5 %collective-permute-start.6 = (bf16[2,512,128]{2,1,0:T(8,128)(2,1)S(1)}, bf16[2,512,128]{2,1,0:T(8,128)(2,1)S(1)}, u32[]{:S(2)}, u32[]{:S(2)}) collective-permute-start(bf16[2,512,128]{2,1,0:T(8,128)(2,1)S(1)} %collective-permute-done.5.refs_4_), channel_id=1, source_target_pairs={{0,4},{4,0},{8,12},{12,8},{16,20},{20,16},{24,28},{28,24},{1,5},{5... | collective-permute-start | bytes 786440 | tf_op jit(solution)/shard_map/ppermute | solution.py:372
  31.5 0.0 collective-permute-done.7.refs_6_
  31.5 0.5 collective-permute-start.8
  32.1 5.1 %collective-permute-done.2.refs_1_ = bf16[2,512,128]{2,1,0:T(8,128)(2,1)S(1)} collective-permute-done((bf16[2,512,128]{2,1,0:T(8,128)(2,1)S(1)}, bf16[2,512,128]{2,1,0:T(8,128)(2,1)S(1)}, u32[]{:S(2)}, u32[]{:S(2)}) %collective-permute-start.2) | collective-permute-done | bytes 262176 | tf_op jit(solution)/shard_map/ppermute | solution.py:372
  37.2 10.1 %collective-permute-start = (bf16[512,128]{1,0:T(8,128)(2,1)S(1)}, bf16[512,128]{1,0:T(8,128)(2,1)S(1)}, u32[]{:S(2)}, u32[]{:S(2)}) collective-permute-start(bf16[512,128]{1,0:T(8,128)(2,1)S(1)} %get-tuple-element.21), channel_id=1, source_target_pairs={{0,16},{4,20},{8,24},{12,28},{16,0},{20,4},{24,8},{28,12},{1,17},{... | collective-permute-start | bytes 393224 | tf_op jit(solution)/shard_map/ppermute | solution.py:372
  47.3 0.0 collective-permute-done.4.refs_3_
  47.3 0.0 collective-permute-start.16
  47.3 1.1 %collective-permute-done.6.refs_5_ = bf16[2,512,128]{2,1,0:T(8,128)(2,1)S(1)} collective-permute-done((bf16[2,512,128]{2,1,0:T(8,128)(2,1)S(1)}, bf16[2,512,128]{2,1,0:T(8,128)(2,1)S(1)}, u32[]{:S(2)}, u32[]{:S(2)}) %collective-permute-start.6) | collective-permute-done | bytes 262176 | tf_op jit(solution)/shard_map/ppermute | solution.py:372
  48.4 1.5 %collective-permute-start.17 = (bf16[512,1024]{1,0:T(8,128)(2,1)S(1)}, bf16[512,1024]{1,0:T(8,128)(2,1)S(1)}, u32[]{:S(2)}, u32[]{:S(2)}) collective-permute-start(bf16[512,1024]{1,0:T(8,128)(2,1)S(1)} %get-tuple-element.34), channel_id=1, source_target_pairs={{0,2},{1,3},{2,0},{3,1},{4,6},{5,7},{6,4},{7,5},{8,10},{9,11},{10,... | collective-permute-start | bytes 3145736 | tf_op jit(solution)/shard_map/ppermute | solution.py:372
  50.0 2.1 %collective-permute-done.8.refs_7_ = bf16[2,512,128]{2,1,0:T(8,128)(2,1)S(1)} collective-permute-done((bf16[2,512,128]{2,1,0:T(8,128)(2,1)S(1)}, bf16[2,512,128]{2,1,0:T(8,128)(2,1)S(1)}, u32[]{:S(2)}, u32[]{:S(2)}) %collective-permute-start.8) | collective-permute-done | bytes 262176 | tf_op jit(solution)/shard_map/ppermute | solution.py:372
  52.0 8.9 %collective-permute-start.13 = (bf16[512,128]{1,0:T(8,128)(2,1)S(1)}, bf16[512,128]{1,0:T(8,128)(2,1)S(1)}, u32[]{:S(2)}, u32[]{:S(2)}) collective-permute-start(bf16[512,128]{1,0:T(8,128)(2,1)S(1)} %get-tuple-element.30), channel_id=1, source_target_pairs={{0,8},{4,12},{8,0},{12,4},{16,24},{20,28},{24,16},{28,20},{1,9},{5... | collective-permute-start | bytes 393224 | tf_op jit(solution)/shard_map/ppermute | solution.py:372
  60.9 1.4 %plan.1 = (s32[16]{0:T(128)S(1)}, s32[16,256]{1,0:T(8,128)S(1)}) custom-call(s32[16]{0:T(128)S(1)} %copy-done, s32[16]{0:T(128)S(1)} %copy-done.1), custom_call_target="tpu_custom_call" | custom-call | tf_op jit(solution)/shard_map/plan/pallas_call | solution.py:97
  62.4 1.7 %shard_map.77 = (bf16[528,128]{1,0:T(8,128)(2,1)S(1)}, bf16[4352,128]{1,0:T(8,128)(2,1)S(1)}, bf16[144,4352]{1,0:T(8,128)(2,1)S(1)}) custom-call(s32[16]{0:T(128)S(1)} %copy-done, s32[16]{0:T(128)S(1)} %get-tuple-element.19.table_ref, s32[16,256]{1,0:T(8,128)S(1)} %get-tuple-element.20.bounds_ref, bf16[512,128]{1,0:T(8,128)(2,1)S(1)} %collective-permute-done.1.q_ref, ...), custom_call_target="tpu_custom_call" | custom-call | tf_op jit(solution)/shard_map/pallas_call | solution.py:262
  64.1 0.0 collective-permute-done.q_ref
  64.2 1.5 %shard_map.78 = bf16[528,128]{1,0:T(8,128)(2,1)S(1)} custom-call(s32[16]{0:T(128)S(1)} %copy-done, s32[16]{0:T(128)S(1)} %get-tuple-element.19.table_ref, s32[16,256]{1,0:T(8,128)S(1)} %get-tuple-element.20.bounds_ref, bf16[512,128]{1,0:T(8,128)(2,1)S(1)} %collective-permute-done.q_ref, bf16[4352,128]{1,0:T(8,128)(2,1)S(1)} %get-tuple-element.27.refs_0_, ...), custom_call_target="tpu_custom_call" | custom-call | tf_op jit(solution)/shard_map/pallas_call | solution.py:262
  65.7 2.2 %collective-permute-start.9 = (bf16[528,128]{1,0:T(8,128)(2,1)S(1)}, bf16[528,128]{1,0:T(8,128)(2,1)S(1)}, u32[]{:S(2)}, u32[]{:S(2)}) collective-permute-start(bf16[528,128]{1,0:T(8,128)(2,1)S(1)} %shard_map.78), channel_id=1, source_target_pairs={{0,16},{4,20},{8,24},{12,28},{16,0},{20,4},{24,8},{28,12},{1,17},{... | collective-permute-start | bytes 405512 | tf_op jit(solution)/shard_map/ppermute | solution.py:372
  67.9 0.0 collective-permute-done.13.q_ref
  67.9 2.6 %shard_map.80 = bf16[528,128]{1,0:T(8,128)(2,1)S(1)} custom-call(s32[16]{0:T(128)S(1)} %copy-done, s32[16]{0:T(128)S(1)} %get-tuple-element.19.table_ref, s32[16,256]{1,0:T(8,128)S(1)} %get-tuple-element.20.bounds_ref, bf16[512,128]{1,0:T(8,128)(2,1)S(1)} %collective-permute-done.13.q_ref, bf16[4352,128]{1,0:T(8,128)(2,1)S(1)} %get-tuple-element.27.refs_0_, ...), custom_call_target="tpu_custom_call" | custom-call | tf_op jit(solution)/shard_map/pallas_call | solution.py:262
  70.5 0.9 collective-permute-start.14
  71.5 1.5 %shard_map.79.refs_0_.refs_4_ = bf16[528,128]{1,0:T(8,128)(2,1)S(1)} custom-call(s32[16]{0:T(128)S(1)} %copy-done, s32[16]{0:T(128)S(1)} %get-tuple-element.19.table_ref, s32[16,256]{1,0:T(8,128)S(1)} %get-tuple-element.20.bounds_ref, bf16[512,128]{1,0:T(8,128)(2,1)S(1)} %get-tuple-element.29.q_ref, bf16[4352,128]{1,0:T(8,128)(2,1)S(1)} %get-tuple-element.27.refs_0_, ...), custom_call_target="tpu_custom_call" | custom-call | tf_op jit(solution)/shard_map/pallas_call | solution.py:262
  73.0 0.0 collective-permute-done.18.refs_15_.refs_10_
  73.0 1.6 %collective-permute-start.21 = (bf16[528,128]{1,0:T(8,128)(2,1)S(1)}, bf16[528,128]{1,0:T(8,128)(2,1)S(1)}, u32[]{:S(2)}, u32[]{:S(2)}) collective-permute-start(bf16[528,128]{1,0:T(8,128)(2,1)S(1)} %shard_map.79.refs_0_.refs_4_), channel_id=1, source_target_pairs={{0,2},{1,3},{2,0},{3,1},{4,6},{5,7},{6,4},{7,5},{8,10},{9,11},{10,... | collective-permute-start | bytes 405512 | tf_op jit(solution)/shard_map/ppermute | solution.py:372
  74.6 0.0 collective-permute-done.9.refs_0_
  74.6 0.0 collective-permute-start.20
  74.6 1.0 collective-permute-done.14.refs_4_.refs_5_
  75.6 1.4 %collective-permute-start.15 = (bf16[528,128]{1,0:T(8,128)(2,1)S(1)}, bf16[528,128]{1,0:T(8,128)(2,1)S(1)}, u32[]{:S(2)}, u32[]{:S(2)}) collective-permute-start(bf16[528,128]{1,0:T(8,128)(2,1)S(1)} %get-tuple-element.31), channel_id=1, source_target_pairs={{0,24},{4,28},{8,16},{12,20},{16,8},{20,12},{24,0},{28,4},{1,25},{... | collective-permute-start | bytes 405512 | tf_op jit(solution)/shard_map/ppermute | solution.py:372
  77.0 1.0 collective-permute-done.21.refs_2_
  78.1 1.5 %collective-permute-start.11 = (bf16[528,128]{1,0:T(8,128)(2,1)S(1)}, bf16[528,128]{1,0:T(8,128)(2,1)S(1)}, u32[]{:S(2)}, u32[]{:S(2)}) collective-permute-start(bf16[528,128]{1,0:T(8,128)(2,1)S(1)} %collective-permute-done.9.refs_0_), channel_id=1, source_target_pairs={{0,2},{1,3},{2,0},{3,1},{4,6},{5,7},{6,4},{7,5},{8,10},{9,11},{10,... | collective-permute-start | bytes 405512 | tf_op jit(solution)/shard_map/ppermute | solution.py:372
  79.6 0.0 collective-permute-done.20.refs_1_
  79.6 0.5 collective-permute-start.24
  80.1 2.4 %collective-permute-done.15.refs_8_.refs_6_ = bf16[528,128]{1,0:T(8,128)(2,1)S(1)} collective-permute-done((bf16[528,128]{1,0:T(8,128)(2,1)S(1)}, bf16[528,128]{1,0:T(8,128)(2,1)S(1)}, u32[]{:S(2)}, u32[]{:S(2)}) %collective-permute-start.15) | collective-permute-done | bytes 135200 | tf_op jit(solution)/shard_map/ppermute | solution.py:372
  82.5 0.0 collective-permute-start.23
  82.5 1.2 %collective-permute-done.11.refs_2_ = bf16[528,128]{1,0:T(8,128)(2,1)S(1)} collective-permute-done((bf16[528,128]{1,0:T(8,128)(2,1)S(1)}, bf16[528,128]{1,0:T(8,128)(2,1)S(1)}, u32[]{:S(2)}, u32[]{:S(2)}) %collective-permute-start.11) | collective-permute-done | bytes 135200 | tf_op jit(solution)/shard_map/ppermute | solution.py:372
  83.7 0.0 collective-permute-start.22
  83.7 1.4 %collective-permute-done.24.refs_6_ = bf16[528,128]{1,0:T(8,128)(2,1)S(1)} collective-permute-done((bf16[528,128]{1,0:T(8,128)(2,1)S(1)}, bf16[528,128]{1,0:T(8,128)(2,1)S(1)}, u32[]{:S(2)}, u32[]{:S(2)}) %collective-permute-start.24) | collective-permute-done | bytes 135200 | tf_op jit(solution)/shard_map/ppermute | solution.py:372
  85.1 4.9 %collective-permute-start.19 = (bf16[256,1024]{1,0:T(8,128)(2,1)S(1)}, bf16[256,1024]{1,0:T(8,128)(2,1)S(1)}, u32[]{:S(2)}, u32[]{:S(2)}) collective-permute-start(bf16[256,1024]{1,0:T(8,128)(2,1)S(1)} %collective-permute-done.18.refs_15_.refs_10_), channel_id=1, source_target_pairs={{0,4},{4,0},{8,12},{12,8},{16,20},{20,16},{24,28},{28,24},{1,5},{5... | collective-permute-start | bytes 1572872 | tf_op jit(solution)/shard_map/ppermute | solution.py:372
  90.0 0.0 collective-permute-done.23.refs_5_
  90.0 0.5 collective-permute-start.27
  90.5 0.0 collective-permute-done.22.refs_3_
  90.5 0.0 collective-permute-start.26
  90.5 4.5 %collective-permute-done.27.refs_10_ = bf16[528,128]{1,0:T(8,128)(2,1)S(1)} collective-permute-done((bf16[528,128]{1,0:T(8,128)(2,1)S(1)}, bf16[528,128]{1,0:T(8,128)(2,1)S(1)}, u32[]{:S(2)}, u32[]{:S(2)}) %collective-permute-start.27) | collective-permute-done | bytes 135200 | tf_op jit(solution)/shard_map/ppermute | solution.py:372
  95.0 0.5 collective-permute-start.28
  95.5 0.8 collective-permute-done.25.refs_7_
  96.4 0.1 collective-permute-start.10
  96.5 0.0 collective-permute-done.28.refs_11_
  96.6 0.3 collective-permute-start.12
  96.9 4.5 %collective-permute-done.19.refs_16_.refs_11_ = bf16[256,1024]{1,0:T(8,128)(2,1)S(1)} collective-permute-done((bf16[256,1024]{1,0:T(8,128)(2,1)S(1)}, bf16[256,1024]{1,0:T(8,128)(2,1)S(1)}, u32[]{:S(2)}, u32[]{:S(2)}) %collective-permute-start.19) | collective-permute-done | bytes 524320 | tf_op jit(solution)/shard_map/ppermute | solution.py:372
  101.4 0.0 collective-permute-done.16.refs_13_.refs_8_
  101.4 1.8 %early.1.refs_12_ = f32[512,1024]{1,0:T(8,128)S(1)} custom-call(bf16[528,128]{1,0:T(8,128)(2,1)S(1)} %shard_map.79.refs_0_.refs_4_, bf16[528,128]{1,0:T(8,128)(2,1)S(1)} %collective-permute-done.20.refs_1_, bf16[528,128]{1,0:T(8,128)(2,1)S(1)} %collective-permute-done.21.refs_2_, bf16[528,128]{1,0:T(8,128)(2,1)S(1)} %collective-permute-done.22.refs_3_, ...), custom_call_target="tpu_custom_call" | custom-call | tf_op jit(solution)/shard_map/early/pallas_call | solution.py:343
  103.2 0.0 collective-permute-done.10.refs_1_
  103.2 0.0 collective-permute-done.12.refs_3_
  103.3 1.7 %late.1 = (bf16[512,1024]{1,0:T(8,128)(2,1)}, f32[4,512]{1,0:T(4,128)}) custom-call(bf16[528,128]{1,0:T(8,128)(2,1)S(1)} %collective-permute-done.9.refs_0_, bf16[528,128]{1,0:T(8,128)(2,1)S(1)} %collective-permute-done.10.refs_1_, bf16[528,128]{1,0:T(8,128)(2,1)S(1)} %collective-permute-done.11.refs_2_, ...), custom_call_target="tpu_custom_call" | custom-call | tf_op jit(solution)/shard_map/late/pallas_call | solution.py:352
  (7 shorter events, 0.0 us)
Async XLA Ops:
  2.3 27.3 %collective-permute-start.3 = (bf16[2,512,128]{2,1,0:T(8,128)(2,1)S(1)}, bf16[2,512,128]{2,1,0:T(8,128)(2,1)S(1)}, u32[]{:S(2)}, u32[]{:S(2)}) collective-permute-start(bf16[2,512,128]{2,1,0:T(8,128)(2,1)S(1)} %get-tuple-element.24), channel_id=1, source_target_pairs={{0,8},{4,12},{8,0},{12,4},{16,24},{20,28},{24,16},{28,20},{1,9},{5... | collective-permute-start | bytes 786440 | tf_op jit(solution)/shard_map/ppermute | solution.py:372
  5.4 24.7 %collective-permute-start.5 = (bf16[2,512,128]{2,1,0:T(8,128)(2,1)S(1)}, bf16[2,512,128]{2,1,0:T(8,128)(2,1)S(1)}, u32[]{:S(2)}, u32[]{:S(2)}) collective-permute-start(bf16[2,512,128]{2,1,0:T(8,128)(2,1)S(1)} %get-tuple-element.25), channel_id=1, source_target_pairs={{0,16},{4,20},{8,24},{12,28},{16,0},{20,4},{24,8},{28,12},{1,17},{... | collective-permute-start | bytes 786440 | tf_op jit(solution)/shard_map/ppermute | solution.py:372
  8.0 23.6 %collective-permute-start.7 = (bf16[2,512,128]{2,1,0:T(8,128)(2,1)S(1)}, bf16[2,512,128]{2,1,0:T(8,128)(2,1)S(1)}, u32[]{:S(2)}, u32[]{:S(2)}) collective-permute-start(bf16[2,512,128]{2,1,0:T(8,128)(2,1)S(1)} %get-tuple-element.26), channel_id=1, source_target_pairs={{0,24},{4,28},{8,16},{12,20},{16,8},{20,12},{24,0},{28,4},{1,25},{... | collective-permute-start | bytes 786440 | tf_op jit(solution)/shard_map/ppermute | solution.py:372
  8.0 53.0 %copy-start = (s32[16]{0:T(128)S(1)}, s32[16]{0:T(128)}, u32[]{:S(2)}) copy-start(s32[16]{0:T(128)} %layout_ref.9) | copy-start | bytes 196
  8.0 53.0 %copy-start.1 = (s32[16]{0:T(128)S(1)}, s32[16]{0:T(128)}, u32[]{:S(2)}) copy-start(s32[16]{0:T(128)} %lens_ref.1) | copy-start | bytes 196
  8.0 20.0 %collective-permute-start.1 = (bf16[512,128]{1,0:T(8,128)(2,1)S(1)}, bf16[512,128]{1,0:T(8,128)(2,1)S(1)}, u32[]{:S(2)}, u32[]{:S(2)}) collective-permute-start(bf16[512,128]{1,0:T(8,128)(2,1)S(1)} %get-tuple-element.22), channel_id=1, source_target_pairs={{0,24},{4,28},{8,16},{12,20},{16,8},{20,12},{24,0},{28,4},{1,25},{... | collective-permute-start | bytes 393224 | tf_op jit(solution)/shard_map/ppermute | solution.py:372
  13.8 59.1 %collective-permute-start.18 = (bf16[256,1024]{1,0:T(8,128)(2,1)S(1)}, bf16[256,1024]{1,0:T(8,128)(2,1)S(1)}, u32[]{:S(2)}, u32[]{:S(2)}) collective-permute-start(bf16[256,1024]{1,0:T(8,128)(2,1)S(1)} %get-tuple-element.35), channel_id=1, source_target_pairs={{0,3},{1,2},{2,1},{3,0},{4,7},{5,6},{6,5},{7,4},{8,11},{9,10},{10,... | collective-permute-start | bytes 1572872 | tf_op jit(solution)/shard_map/ppermute | solution.py:372
  28.0 9.2 %collective-permute-start.2 = (bf16[2,512,128]{2,1,0:T(8,128)(2,1)S(1)}, bf16[2,512,128]{2,1,0:T(8,128)(2,1)S(1)}, u32[]{:S(2)}, u32[]{:S(2)}) collective-permute-start(bf16[2,512,128]{2,1,0:T(8,128)(2,1)S(1)} %get-tuple-element.23.refs_0_), channel_id=1, source_target_pairs={{0,4},{4,0},{8,12},{12,8},{16,20},{20,16},{24,28},{28,24},{1,5},{5... | collective-permute-start | bytes 786440 | tf_op jit(solution)/shard_map/ppermute | solution.py:372
  29.5 17.8 %collective-permute-start.4 = (bf16[2,512,128]{2,1,0:T(8,128)(2,1)S(1)}, bf16[2,512,128]{2,1,0:T(8,128)(2,1)S(1)}, u32[]{:S(2)}, u32[]{:S(2)}) collective-permute-start(bf16[2,512,128]{2,1,0:T(8,128)(2,1)S(1)} %collective-permute-done.3.refs_2_), channel_id=1, source_target_pairs={{0,4},{4,0},{8,12},{12,8},{16,20},{20,16},{24,28},{28,24},{1,5},{5... | collective-permute-start | bytes 786440 | tf_op jit(solution)/shard_map/ppermute | solution.py:372
  30.1 18.4 %collective-permute-start.6 = (bf16[2,512,128]{2,1,0:T(8,128)(2,1)S(1)}, bf16[2,512,128]{2,1,0:T(8,128)(2,1)S(1)}, u32[]{:S(2)}, u32[]{:S(2)}) collective-permute-start(bf16[2,512,128]{2,1,0:T(8,128)(2,1)S(1)} %collective-permute-done.5.refs_4_), channel_id=1, source_target_pairs={{0,4},{4,0},{8,12},{12,8},{16,20},{20,16},{24,28},{28,24},{1,5},{5... | collective-permute-start | bytes 786440 | tf_op jit(solution)/shard_map/ppermute | solution.py:372
  31.5 20.5 %collective-permute-start.8 = (bf16[2,512,128]{2,1,0:T(8,128)(2,1)S(1)}, bf16[2,512,128]{2,1,0:T(8,128)(2,1)S(1)}, u32[]{:S(2)}, u32[]{:S(2)}) collective-permute-start(bf16[2,512,128]{2,1,0:T(8,128)(2,1)S(1)} %collective-permute-done.7.refs_6_), channel_id=1, source_target_pairs={{0,4},{4,0},{8,12},{12,8},{16,20},{20,16},{24,28},{28,24},{1,5},{5... | collective-permute-start | bytes 786440 | tf_op jit(solution)/shard_map/ppermute | solution.py:372
  37.2 26.9 %collective-permute-start = (bf16[512,128]{1,0:T(8,128)(2,1)S(1)}, bf16[512,128]{1,0:T(8,128)(2,1)S(1)}, u32[]{:S(2)}, u32[]{:S(2)}) collective-permute-start(bf16[512,128]{1,0:T(8,128)(2,1)S(1)} %get-tuple-element.21), channel_id=1, source_target_pairs={{0,16},{4,20},{8,24},{12,28},{16,0},{20,4},{24,8},{28,12},{1,17},{... | collective-permute-start | bytes 393224 | tf_op jit(solution)/shard_map/ppermute | solution.py:372
  47.3 54.1 %collective-permute-start.16 = (bf16[512,1024]{1,0:T(8,128)(2,1)S(1)}, bf16[512,1024]{1,0:T(8,128)(2,1)S(1)}, u32[]{:S(2)}, u32[]{:S(2)}) collective-permute-start(bf16[512,1024]{1,0:T(8,128)(2,1)S(1)} %get-tuple-element.33), channel_id=1, source_target_pairs={{0,1},{1,0},{2,3},{3,2},{4,5},{5,4},{6,7},{7,6},{8,9},{9,8},{10,11... | collective-permute-start | bytes 3145736 | tf_op jit(solution)/shard_map/ppermute | solution.py:372
  48.4 53.0 %collective-permute-start.17 = (bf16[512,1024]{1,0:T(8,128)(2,1)S(1)}, bf16[512,1024]{1,0:T(8,128)(2,1)S(1)}, u32[]{:S(2)}, u32[]{:S(2)}) collective-permute-start(bf16[512,1024]{1,0:T(8,128)(2,1)S(1)} %get-tuple-element.34), channel_id=1, source_target_pairs={{0,2},{1,3},{2,0},{3,1},{4,6},{5,7},{6,4},{7,5},{8,10},{9,11},{10,... | collective-permute-start | bytes 3145736 | tf_op jit(solution)/shard_map/ppermute | solution.py:372
  52.0 15.9 %collective-permute-start.13 = (bf16[512,128]{1,0:T(8,128)(2,1)S(1)}, bf16[512,128]{1,0:T(8,128)(2,1)S(1)}, u32[]{:S(2)}, u32[]{:S(2)}) collective-permute-start(bf16[512,128]{1,0:T(8,128)(2,1)S(1)} %get-tuple-element.30), channel_id=1, source_target_pairs={{0,8},{4,12},{8,0},{12,4},{16,24},{20,28},{24,16},{28,20},{1,9},{5... | collective-permute-start | bytes 393224 | tf_op jit(solution)/shard_map/ppermute | solution.py:372
  65.7 8.9 %collective-permute-start.9 = (bf16[528,128]{1,0:T(8,128)(2,1)S(1)}, bf16[528,128]{1,0:T(8,128)(2,1)S(1)}, u32[]{:S(2)}, u32[]{:S(2)}) collective-permute-start(bf16[528,128]{1,0:T(8,128)(2,1)S(1)} %shard_map.78), channel_id=1, source_target_pairs={{0,16},{4,20},{8,24},{12,28},{16,0},{20,4},{24,8},{28,12},{1,17},{... | collective-permute-start | bytes 405512 | tf_op jit(solution)/shard_map/ppermute | solution.py:372
  70.5 5.1 %collective-permute-start.14 = (bf16[528,128]{1,0:T(8,128)(2,1)S(1)}, bf16[528,128]{1,0:T(8,128)(2,1)S(1)}, u32[]{:S(2)}, u32[]{:S(2)}) collective-permute-start(bf16[528,128]{1,0:T(8,128)(2,1)S(1)} %shard_map.80), channel_id=1, source_target_pairs={{0,8},{4,12},{8,0},{12,4},{16,24},{20,28},{24,16},{28,20},{1,9},{5... | collective-permute-start | bytes 405512 | tf_op jit(solution)/shard_map/ppermute | solution.py:372
  73.0 5.1 %collective-permute-start.21 = (bf16[528,128]{1,0:T(8,128)(2,1)S(1)}, bf16[528,128]{1,0:T(8,128)(2,1)S(1)}, u32[]{:S(2)}, u32[]{:S(2)}) collective-permute-start(bf16[528,128]{1,0:T(8,128)(2,1)S(1)} %shard_map.79.refs_0_.refs_4_), channel_id=1, source_target_pairs={{0,2},{1,3},{2,0},{3,1},{4,6},{5,7},{6,4},{7,5},{8,10},{9,11},{10,... | collective-permute-start | bytes 405512 | tf_op jit(solution)/shard_map/ppermute | solution.py:372
  74.6 5.0 %collective-permute-start.20 = (bf16[528,128]{1,0:T(8,128)(2,1)S(1)}, bf16[528,128]{1,0:T(8,128)(2,1)S(1)}, u32[]{:S(2)}, u32[]{:S(2)}) collective-permute-start(bf16[528,128]{1,0:T(8,128)(2,1)S(1)} %shard_map.79.refs_0_.refs_4_), channel_id=1, source_target_pairs={{0,1},{1,0},{2,3},{3,2},{4,5},{5,4},{6,7},{7,6},{8,9},{9,8},{10,11... | collective-permute-start | bytes 405512 | tf_op jit(solution)/shard_map/ppermute | solution.py:372
  75.6 6.9 %collective-permute-start.15 = (bf16[528,128]{1,0:T(8,128)(2,1)S(1)}, bf16[528,128]{1,0:T(8,128)(2,1)S(1)}, u32[]{:S(2)}, u32[]{:S(2)}) collective-permute-start(bf16[528,128]{1,0:T(8,128)(2,1)S(1)} %get-tuple-element.31), channel_id=1, source_target_pairs={{0,24},{4,28},{8,16},{12,20},{16,8},{20,12},{24,0},{28,4},{1,25},{... | collective-permute-start | bytes 405512 | tf_op jit(solution)/shard_map/ppermute | solution.py:372
  78.1 5.6 %collective-permute-start.11 = (bf16[528,128]{1,0:T(8,128)(2,1)S(1)}, bf16[528,128]{1,0:T(8,128)(2,1)S(1)}, u32[]{:S(2)}, u32[]{:S(2)}) collective-permute-start(bf16[528,128]{1,0:T(8,128)(2,1)S(1)} %collective-permute-done.9.refs_0_), channel_id=1, source_target_pairs={{0,2},{1,3},{2,0},{3,1},{4,6},{5,7},{6,4},{7,5},{8,10},{9,11},{10,... | collective-permute-start | bytes 405512 | tf_op jit(solution)/shard_map/ppermute | solution.py:372
  79.6 5.5 %collective-permute-start.24 = (bf16[528,128]{1,0:T(8,128)(2,1)S(1)}, bf16[528,128]{1,0:T(8,128)(2,1)S(1)}, u32[]{:S(2)}, u32[]{:S(2)}) collective-permute-start(bf16[528,128]{1,0:T(8,128)(2,1)S(1)} %collective-permute-done.14.refs_4_.refs_5_), channel_id=1, source_target_pairs={{0,2},{1,3},{2,0},{3,1},{4,6},{5,7},{6,4},{7,5},{8,10},{9,11},{10,... | collective-permute-start | bytes 405512 | tf_op jit(solution)/shard_map/ppermute | solution.py:372
  82.5 7.5 %collective-permute-start.23 = (bf16[528,128]{1,0:T(8,128)(2,1)S(1)}, bf16[528,128]{1,0:T(8,128)(2,1)S(1)}, u32[]{:S(2)}, u32[]{:S(2)}) collective-permute-start(bf16[528,128]{1,0:T(8,128)(2,1)S(1)} %collective-permute-done.14.refs_4_.refs_5_), channel_id=1, source_target_pairs={{0,1},{1,0},{2,3},{3,2},{4,5},{5,4},{6,7},{7,6},{8,9},{9,8},{10,11... | collective-permute-start | bytes 405512 | tf_op jit(solution)/shard_map/ppermute | solution.py:372
  83.7 6.9 %collective-permute-start.22 = (bf16[528,128]{1,0:T(8,128)(2,1)S(1)}, bf16[528,128]{1,0:T(8,128)(2,1)S(1)}, u32[]{:S(2)}, u32[]{:S(2)}) collective-permute-start(bf16[528,128]{1,0:T(8,128)(2,1)S(1)} %collective-permute-done.21.refs_2_), channel_id=1, source_target_pairs={{0,1},{1,0},{2,3},{3,2},{4,5},{5,4},{6,7},{7,6},{8,9},{9,8},{10,11... | collective-permute-start | bytes 405512 | tf_op jit(solution)/shard_map/ppermute | solution.py:372
  85.1 16.3 %collective-permute-start.19 = (bf16[256,1024]{1,0:T(8,128)(2,1)S(1)}, bf16[256,1024]{1,0:T(8,128)(2,1)S(1)}, u32[]{:S(2)}, u32[]{:S(2)}) collective-permute-start(bf16[256,1024]{1,0:T(8,128)(2,1)S(1)} %collective-permute-done.18.refs_15_.refs_10_), channel_id=1, source_target_pairs={{0,4},{4,0},{8,12},{12,8},{16,20},{20,16},{24,28},{28,24},{1,5},{5... | collective-permute-start | bytes 1572872 | tf_op jit(solution)/shard_map/ppermute | solution.py:372
  90.0 5.0 %collective-permute-start.27 = (bf16[528,128]{1,0:T(8,128)(2,1)S(1)}, bf16[528,128]{1,0:T(8,128)(2,1)S(1)}, u32[]{:S(2)}, u32[]{:S(2)}) collective-permute-start(bf16[528,128]{1,0:T(8,128)(2,1)S(1)} %collective-permute-done.15.refs_8_.refs_6_), channel_id=1, source_target_pairs={{0,2},{1,3},{2,0},{3,1},{4,6},{5,7},{6,4},{7,5},{8,10},{9,11},{10,... | collective-permute-start | bytes 405512 | tf_op jit(solution)/shard_map/ppermute | solution.py:372
  90.5 4.5 %collective-permute-start.26 = (bf16[528,128]{1,0:T(8,128)(2,1)S(1)}, bf16[528,128]{1,0:T(8,128)(2,1)S(1)}, u32[]{:S(2)}, u32[]{:S(2)}) collective-permute-start(bf16[528,128]{1,0:T(8,128)(2,1)S(1)} %collective-permute-done.15.refs_8_.refs_6_), channel_id=1, source_target_pairs={{0,1},{1,0},{2,3},{3,2},{4,5},{5,4},{6,7},{7,6},{8,9},{9,8},{10,11... | collective-permute-start | bytes 405512 | tf_op jit(solution)/shard_map/ppermute | solution.py:372
  95.0 1.4 %collective-permute-start.25 = (bf16[528,128]{1,0:T(8,128)(2,1)S(1)}, bf16[528,128]{1,0:T(8,128)(2,1)S(1)}, u32[]{:S(2)}, u32[]{:S(2)}) collective-permute-start(bf16[528,128]{1,0:T(8,128)(2,1)S(1)} %collective-permute-done.24.refs_6_), channel_id=1, source_target_pairs={{0,1},{1,0},{2,3},{3,2},{4,5},{5,4},{6,7},{7,6},{8,9},{9,8},{10,11... | collective-permute-start | bytes 405512 | tf_op jit(solution)/shard_map/ppermute | solution.py:372
  95.0 1.5 %collective-permute-start.28 = (bf16[528,128]{1,0:T(8,128)(2,1)S(1)}, bf16[528,128]{1,0:T(8,128)(2,1)S(1)}, u32[]{:S(2)}, u32[]{:S(2)}) collective-permute-start(bf16[528,128]{1,0:T(8,128)(2,1)S(1)} %collective-permute-done.27.refs_10_), channel_id=1, source_target_pairs={{0,1},{1,0},{2,3},{3,2},{4,5},{5,4},{6,7},{7,6},{8,9},{9,8},{10,11... | collective-permute-start | bytes 405512 | tf_op jit(solution)/shard_map/ppermute | solution.py:372
  96.4 6.9 %collective-permute-start.10 = (bf16[528,128]{1,0:T(8,128)(2,1)S(1)}, bf16[528,128]{1,0:T(8,128)(2,1)S(1)}, u32[]{:S(2)}, u32[]{:S(2)}) collective-permute-start(bf16[528,128]{1,0:T(8,128)(2,1)S(1)} %collective-permute-done.9.refs_0_), channel_id=1, source_target_pairs={{0,1},{1,0},{2,3},{3,2},{4,5},{5,4},{6,7},{7,6},{8,9},{9,8},{10,11... | collective-permute-start | bytes 405512 | tf_op jit(solution)/shard_map/ppermute | solution.py:372
  96.6 6.7 %collective-permute-start.12 = (bf16[528,128]{1,0:T(8,128)(2,1)S(1)}, bf16[528,128]{1,0:T(8,128)(2,1)S(1)}, u32[]{:S(2)}, u32[]{:S(2)}) collective-permute-start(bf16[528,128]{1,0:T(8,128)(2,1)S(1)} %collective-permute-done.11.refs_2_), channel_id=1, source_target_pairs={{0,1},{1,0},{2,3},{3,2},{4,5},{5,4},{6,7},{7,6},{8,9},{9,8},{10,11... | collective-permute-start | bytes 405512 | tf_op jit(solution)/shard_map/ppermute | solution.py:372

commit v2 on v1

--- a/solution.py
+++ b/solution.py
@@ -12,9 +12,12 @@
 NEG = -1e30
 LOG_ROWS = 16
 ONES = 16
+UNROLL = 4
+AHEAD = 3
+SLOTS = 4
 LONE, LAST = 3, 2
 PACK_ORDER = (3, 1, 0, 2)
-ATTEND_ORDER = (3, 1, 2, 0)
+ATTEND_ORDER = (0, 3, 1, 2)
 
 
 HBM_SPEC = pl.BlockSpec(memory_space=pltpu.MemorySpace.HBM)
@@ -145,41 +148,66 @@
     )(pltpu.with_memory_space_constraint(weight, pltpu.HBM))
 
 
-def attention_kernel(place, places, spread, layout_ref, table_ref, bounds_ref, q_ref, *refs):
+def place_chunk(chunk, owner, layout_ref, k_all, v_all):
+    half = chunk.shape[1] // 2
+    for b in range(2):
+        first = pl.multiple_of(layout_ref[owner * 2 + b] * half, half)
+        k_all[pl.ds(first, half), :] = chunk[0, b * half : (b + 1) * half, :]
+        for i in range(0, half, HEAD_DIM):
+            columns = pl.ds(pl.multiple_of(first + i, HEAD_DIM), HEAD_DIM)
+            v_all[:HEAD_DIM, columns] = chunk[1, b * half + i : b * half + i + HEAD_DIM, :]
+
+
+def owner_of(s, t, spread):
+    me = lax.axis_index("ctx")
+    return (me // spread ^ s) * spread + (me % spread + spread - t) % spread
+
+
+def sort_kernel(sources, spread, layout_ref, *refs):
+    chunks, (k_all, v_all) = refs[:-2], refs[-2:]
+    for chunk, (s, t) in zip(chunks, sources):
+        place_chunk(chunk, owner_of(s, t, spread), layout_ref, k_all, v_all)
+    half = chunks[0].shape[1] // 2
+    total = layout_ref.shape[0] * half
+    k_all[total:, :] = jnp.zeros((half, HEAD_DIM), k_all.dtype)
+    v_all[:HEAD_DIM, total:] = jnp.zeros((HEAD_DIM, half), v_all.dtype)
+    v_all[HEAD_DIM:, :] = jnp.ones((ONES, total + half), v_all.dtype)
+
+
+def sort(layout, chunks, sources, spread):
+    rows = chunks[0].shape[1]
+    long = layout.shape[0] * (rows // 2) + rows // 2
+    return pl.pallas_call(
+        functools.partial(sort_kernel, sources, spread),
+        out_shape=[
+            jax.ShapeDtypeStruct((long, HEAD_DIM), jnp.bfloat16),
+            jax.ShapeDtypeStruct((HEAD_DIM + ONES, long), jnp.bfloat16),
+        ],
+        in_specs=[SMEM_SPEC] + [VMEM_SPEC] * len(chunks),
+        out_specs=[VMEM_SPEC] * 2,
+        compiler_params=pltpu.CompilerParams(vmem_limit_bytes=24 * MIB),
+        name="sort",
+    )(layout, *chunks)
+
+
+def attention_kernel(place, places, spread, sources, layout_ref, table_ref, bounds_ref, q_ref, *refs):
     refs, (scores, peaks, tops, summed) = refs[:-4], refs[-4:]
-    sort = len(refs) != 3
-    if sort:
-        kv_refs, (out_ref, k_all, v_all) = refs[:-3], refs[-3:]
+    late = refs[2:-3] if len(refs) != 3 else ()
+    if late:
+        out_ref, k_all, v_all = refs[-3:]
     else:
         k_all, v_all, out_ref = refs
     rows = q_ref.shape[0]
     half = rows // 2
-    width = 2 * half
+    width = half
     factor = math.log2(math.e) / math.sqrt(HEAD_DIM)
 
-    if sort:
-        me = lax.axis_index("ctx")
-        z, r = me // spread, me % spread
-        for s in range(places):
-            for t in range(spread):
-                owner = (z ^ s) * spread + (r + spread - t) % spread
-                chunk = kv_refs[s * spread + t]
-                for b in range(2):
-                    first = pl.multiple_of(layout_ref[owner * 2 + b] * half, half)
-                    k_all[pl.ds(first, half), :] = chunk[0, b * half : (b + 1) * half, :]
-                    for i in range(0, half, HEAD_DIM):
-                        columns = pl.ds(pl.multiple_of(first + i, HEAD_DIM), HEAD_DIM)
-                        v_all[:HEAD_DIM, columns] = chunk[
-                            1, b * half + i : b * half + i + HEAD_DIM, :
-                        ]
-        total = layout_ref.shape[0] * half
-        k_all[total:, :] = jnp.zeros((half, HEAD_DIM), k_all.dtype)
-        v_all[:HEAD_DIM, total:] = jnp.zeros((HEAD_DIM, half), v_all.dtype)
-        v_all[HEAD_DIM:, :] = jnp.ones((ONES, total + half), v_all.dtype)
+    for chunk, (s, t) in zip(late, sources):
+        place_chunk(chunk, owner_of(s, t, spread), layout_ref, k_all, v_all)
 
     blocks = [table_ref[4 * place + 2 * b] for b in range(2)]
     lows = [table_ref[4 * place + 2 * b + 1] for b in range(2)]
-    counts = [(blocks[b] - lows[b] + 2) // 2 for b in range(2)]
+    counts = [blocks[b] - lows[b] + 1 for b in range(2)]
     items = counts[0] + counts[1]
     key_row = lax.broadcasted_iota(jnp.int32, (width, half), 0)
     tops[...] = jnp.full(tops.shape, NEG, jnp.float32)
@@ -189,7 +217,7 @@
         late = jnp.logical_and(item >= counts[0], item < items).astype(jnp.int32)
         low = jnp.where(late == 1, lows[1], lows[0])
         step = jnp.where(item < items, item - late * counts[0], 0)
-        base = pl.multiple_of((low + 2 * step) * half, half)
+        base = pl.multiple_of((low + step) * half, half)
         return late, base
 
     def score(item, slot):
@@ -220,16 +248,16 @@
             preferred_element_type=jnp.float32,
         )
 
-    score(0, 0)
-
-    def pair(i, carry):
-        score(2 * i + 1, 1)
-        absorb(2 * i, 0)
-        score(2 * i + 2, 0)
-        absorb(2 * i + 1, 1)
+    for j in range(AHEAD):
+        score(j, j)
+
+    def batch(i, carry):
+        for j in range(UNROLL):
+            score(UNROLL * i + j + AHEAD, (j + AHEAD) % SLOTS)
+            absorb(UNROLL * i + j, j % SLOTS)
         return carry
 
-    lax.fori_loop(0, (items + 1) // 2, pair, 0)
+    lax.fori_loop(0, (items + UNROLL - 1) // UNROLL, batch, 0)
 
     log_rows = []
     for b in range(2):
@@ -248,30 +276,26 @@
     out_ref[pl.ds(rows, LOG_ROWS), :] = jnp.concatenate(split, axis=0).astype(jnp.bfloat16)
 
 
-def attend(layout, table, bounds, query, sources, place, places, spread):
+def attend(layout, table, bounds, query, whole, late, sources, place, places, spread):
     rows = query.shape[0]
     half = rows // 2
-    total = layout.shape[0] * half
-    first = len(sources) != 2
     out_shape = [jax.ShapeDtypeStruct((rows + LOG_ROWS, HEAD_DIM), jnp.bfloat16)]
-    if first:
-        out_shape += [
-            jax.ShapeDtypeStruct((total + half, HEAD_DIM), jnp.bfloat16),
-            jax.ShapeDtypeStruct((HEAD_DIM + ONES, total + half), jnp.bfloat16),
-        ]
-    return pl.pallas_call(
-        functools.partial(attention_kernel, place, places, spread),
+    if late:
+        out_shape += [jax.ShapeDtypeStruct(x.shape, x.dtype) for x in whole]
+    return pl.pallas_call(
+        functools.partial(attention_kernel, place, places, spread, sources),
         out_shape=out_shape,
-        in_specs=[SMEM_SPEC] * 2 + [VMEM_SPEC] * (2 + len(sources)),
+        in_specs=[SMEM_SPEC] * 2 + [VMEM_SPEC] * (4 + len(late)),
         out_specs=[VMEM_SPEC] * len(out_shape),
+        input_output_aliases={4: 1, 5: 2} if late else {},
         scratch_shapes=[
-            pltpu.VMEM((2, 2 * half, half), jnp.float32),
-            pltpu.VMEM((2, 1, half), jnp.float32),
+            pltpu.VMEM((SLOTS, half, half), jnp.float32),
+            pltpu.VMEM((SLOTS, 1, half), jnp.float32),
             pltpu.VMEM((2, 1, half), jnp.float32),
             pltpu.VMEM((2, HEAD_DIM + ONES, half), jnp.float32),
         ],
         compiler_params=pltpu.CompilerParams(vmem_limit_bytes=24 * MIB),
-    )(layout, table, bounds, query, *sources)
+    )(layout, table, bounds, query, *whole, *late)
 
 
 def weight_rows(w_refs, m, z, side, s, pair):
@@ -315,8 +339,8 @@
 
 
 def late_kernel(places, spread, tp, *refs):
-    parts, logs_in, w_refs = refs[:tp], refs[tp : tp + places - 1], refs[tp + places - 1 : -3]
-    early_ref, out_ref, log_ref = refs[-3:]
+    parts, logs_in, w_refs = refs[:tp], refs[tp : tp + places - 1], refs[tp + places - 1 :]
+    w_refs, (early_ref, out_ref, log_ref) = w_refs[:-3], refs[-3:]
     rows = out_ref.shape[0]
     me = lax.axis_index("ctx")
     z, side = me // spread, me % 2
@@ -383,20 +407,25 @@
     packed = pack(keys, values, queries, places, spread)
     kv, q = packed[:places], packed[places:]
     q = [q[0]] + [over_places(q[s], s) for s in range(1, places)]
-    sources = []
+    chunks = {}
     for s in range(places):
-        sources.append(over_places(kv[s], s) if s else kv[0])
-        sources += [over_spread(sources[-1], t) for t in range(1, spread)]
+        chunks[s, 0] = over_places(kv[s], s) if s else kv[0]
+        for t in range(1, spread):
+            chunks[s, t] = over_spread(chunks[s, 0], t)
 
     packed_weight = pack_weight(out_weight, tp)
     weights = [packed_weight[0]] + [over_tp(packed_weight[m], m) for m in range(1, tp)]
     weights.append(move(weights[-1], "ctx", lambda i: i ^ 1))
 
     table, bounds = plan(layout, doc_lengths, places, spread, keys.shape[0] // 2)
+    late = [(LAST, t) for t in range(1, spread)]
+    soon = [source for source in chunks if source not in late]
+    whole = sort(layout, [chunks[source] for source in soon], soon, spread)
     heads = [None] * places
     for s in ATTEND_ORDER:
-        message, *rest = attend(layout, table, bounds, q[s], sources, s, places, spread)
-        sources = rest or sources
+        extra = [chunks[source] for source in late]
+        message, *rest = attend(layout, table, bounds, q[s], whole, extra, late, s, places, spread)
+        whole, late = rest or whole, []
         heads[s] = over_places(message, s) if s else message
 
     groups = [heads]

time: 105 us -> 105 us (level)
  starting transfers between devices: 48.8 us -> 31.2 us
  waiting for transfers between devices: 39.4 us -> 56.5 us
    ppermute x29, starting transfers between devices: 48.8 us -> 31.2 us  [move(): return lax.ppermute(array, axis, [(i, target(i)) for i in range(count)])]
    ppermute x29, waiting for transfers between devices: 39.4 us -> 56.5 us  [move(): return lax.ppermute(array, axis, [(i, target(i)) for i in range(count)])]
    pallas_call x4 -> x5, Pallas kernels: 7.38 us -> 7.64 us  [the longest x4 6.84 us: attend(): pl.pallas_call(functools.partial(attention_kernel, place, places, spread,...]
where the time goes in v2:
time: 105 us
  waiting for transfers between devices  56.5 us (54%)
  starting transfers between devices  31.2 us (30%)
  Pallas kernels  16.3 us (16%)
    ppermute x29, waiting for transfers between devices, move(): return lax.ppermute(array, axis, [(i, target(i)) for i in range(count)])  56.5 us
    ppermute x29, starting transfers between devices, move(): return lax.ppermute(array, axis, [(i, target(i)) for i in range(count)])  31.2 us
    pallas_call x4, Pallas kernels, attend(): pl.pallas_call(functools.partial(attention_kernel, place, places, spread,...  6.84 us
  transfers between devices with their start and end apart: 29, of which 12 were waited for; matrix products, arithmetic and copies ran while one was open for 0% of the time, Pallas kernels for 12%

profile of v2, /device:TPU:0, one launch (start us, length us, event | category | flops | bytes accessed | tf_op | source)
XLA Modules:
  0.0 104.8 jit_solution(14268574486177935469)
XLA Ops:
  0.6 1.6 %pack.1 = (bf16[2,512,128]{2,1,0:T(8,128)(2,1)S(1)}, bf16[2,512,128]{2,1,0:T(8,128)(2,1)S(1)}, bf16[2,512,128]{2,1,0:T(8,128)(2,1)S(1)}, bf16[2,512,128]{2,1,0:T...) custom-call(bf16[512,512]{1,0:T(8,128)(2,1)} %k_ref.1, ...), custom_call_target="tpu_custom_call" | custom-call | tf_op jit(solution)/shard_map/pack/pallas_call | solution.py:57
  2.3 3.1 %collective-permute-start.2 = (bf16[2,512,128]{2,1,0:T(8,128)(2,1)S(1)}, bf16[2,512,128]{2,1,0:T(8,128)(2,1)S(1)}, u32[]{:S(2)}, u32[]{:S(2)}) collective-permute-start(bf16[2,512,128]{2,1,0:T(8,128)(2,1)S(1)} %get-tuple-element.26), channel_id=1, source_target_pairs={{0,8},{4,12},{8,0},{12,4},{16,24},{20,28},{24,16},{28,20},{1,9},{5... | collective-permute-start | bytes 786440 | tf_op jit(solution)/shard_map/ppermute | solution.py:396
  5.4 2.6 %collective-permute-start.4 = (bf16[2,512,128]{2,1,0:T(8,128)(2,1)S(1)}, bf16[2,512,128]{2,1,0:T(8,128)(2,1)S(1)}, u32[]{:S(2)}, u32[]{:S(2)}) collective-permute-start(bf16[2,512,128]{2,1,0:T(8,128)(2,1)S(1)} %get-tuple-element.27), channel_id=1, source_target_pairs={{0,16},{4,20},{8,24},{12,28},{16,0},{20,4},{24,8},{28,12},{1,17},{... | collective-permute-start | bytes 786440 | tf_op jit(solution)/shard_map/ppermute | solution.py:396
  8.0 0.0 collective-permute-start.5
  8.0 1.9 %collective-permute-start = (bf16[512,128]{1,0:T(8,128)(2,1)S(1)}, bf16[512,128]{1,0:T(8,128)(2,1)S(1)}, u32[]{:S(2)}, u32[]{:S(2)}) collective-permute-start(bf16[512,128]{1,0:T(8,128)(2,1)S(1)} %get-tuple-element.23), channel_id=1, source_target_pairs={{0,16},{4,20},{8,24},{12,28},{16,0},{20,4},{24,8},{28,12},{1,17},{... | collective-permute-start | bytes 393224 | tf_op jit(solution)/shard_map/ppermute | solution.py:396
  9.9 2.0 %pack_weight.1 = (bf16[512,1024]{1,0:T(8,128)(2,1)S(1)}, bf16[512,1024]{1,0:T(8,128)(2,1)S(1)}, bf16[512,1024]{1,0:T(8,128)(2,1)S(1)}, bf16[256,1024]{1,0:T(8,128)(2,1)S(1)}) custom-call(bf16[512,4096]{1,0:T(8,128)(2,1)} %w_ref.1), custom_call_target="tpu_custom_call" | custom-call | tf_op jit(solution)/shard_map/pack_weight/pallas_call | solution.py:137
  11.9 0.1 collective-permute-start.18
  12.0 24.6 %collective-permute-done.q_ref = bf16[512,128]{1,0:T(8,128)(2,1)S(1)} collective-permute-done((bf16[512,128]{1,0:T(8,128)(2,1)S(1)}, bf16[512,128]{1,0:T(8,128)(2,1)S(1)}, u32[]{:S(2)}, u32[]{:S(2)}) %collective-permute-start) | collective-permute-done | bytes 131104 | tf_op jit(solution)/shard_map/ppermute | solution.py:396
  36.6 1.5 %collective-permute-start.1 = (bf16[2,512,128]{2,1,0:T(8,128)(2,1)S(1)}, bf16[2,512,128]{2,1,0:T(8,128)(2,1)S(1)}, u32[]{:S(2)}, u32[]{:S(2)}) collective-permute-start(bf16[2,512,128]{2,1,0:T(8,128)(2,1)S(1)} %get-tuple-element.25.refs_0_), channel_id=1, source_target_pairs={{0,4},{4,0},{8,12},{12,8},{16,20},{20,16},{24,28},{28,24},{1,5},{5... | collective-permute-start | bytes 786440 | tf_op jit(solution)/shard_map/ppermute | solution.py:396
  38.1 0.0 collective-permute-done.2.refs_2_
  38.1 0.5 collective-permute-start.3
  38.6 0.0 collective-permute-done.4.refs_4_
  38.6 1.5 %collective-permute-start.7 = (bf16[2,512,128]{2,1,0:T(8,128)(2,1)S(1)}, bf16[2,512,128]{2,1,0:T(8,128)(2,1)S(1)}, u32[]{:S(2)}, u32[]{:S(2)}) collective-permute-start(bf16[2,512,128]{2,1,0:T(8,128)(2,1)S(1)} %collective-permute-done.4.refs_4_), channel_id=1, source_target_pairs={{0,4},{4,0},{8,12},{12,8},{16,20},{20,16},{24,28},{28,24},{1,5},{5... | collective-permute-start | bytes 786440 | tf_op jit(solution)/shard_map/ppermute | solution.py:396
  40.1 0.0 collective-permute-done.5.refs_5_
  40.1 0.5 collective-permute-start.6
  40.6 5.1 %collective-permute-done.1.refs_1_ = bf16[2,512,128]{2,1,0:T(8,128)(2,1)S(1)} collective-permute-done((bf16[2,512,128]{2,1,0:T(8,128)(2,1)S(1)}, bf16[2,512,128]{2,1,0:T(8,128)(2,1)S(1)}, u32[]{:S(2)}, u32[]{:S(2)}) %collective-permute-start.1) | collective-permute-done | bytes 262176 | tf_op jit(solution)/shard_map/ppermute | solution.py:396
  45.7 0.0 collective-permute-start.12
  45.7 5.6 %collective-permute-done.3.refs_3_ = bf16[2,512,128]{2,1,0:T(8,128)(2,1)S(1)} collective-permute-done((bf16[2,512,128]{2,1,0:T(8,128)(2,1)S(1)}, bf16[2,512,128]{2,1,0:T(8,128)(2,1)S(1)}, u32[]{:S(2)}, u32[]{:S(2)}) %collective-permute-start.3) | collective-permute-done | bytes 262176 | tf_op jit(solution)/shard_map/ppermute | solution.py:396
  51.4 0.0 collective-permute-start.16
  51.4 5.6 %collective-permute-done.7.refs_2_ = bf16[2,512,128]{2,1,0:T(8,128)(2,1)S(1)} collective-permute-done((bf16[2,512,128]{2,1,0:T(8,128)(2,1)S(1)}, bf16[2,512,128]{2,1,0:T(8,128)(2,1)S(1)}, u32[]{:S(2)}, u32[]{:S(2)}) %collective-permute-start.7) | collective-permute-done | bytes 262176 | tf_op jit(solution)/shard_map/ppermute | solution.py:396
  57.0 1.5 %collective-permute-start.17 = (bf16[512,1024]{1,0:T(8,128)(2,1)S(1)}, bf16[512,1024]{1,0:T(8,128)(2,1)S(1)}, u32[]{:S(2)}, u32[]{:S(2)}) collective-permute-start(bf16[512,1024]{1,0:T(8,128)(2,1)S(1)} %get-tuple-element.38), channel_id=1, source_target_pairs={{0,2},{1,3},{2,0},{3,1},{4,6},{5,7},{6,4},{7,5},{8,10},{9,11},{10,... | collective-permute-start | bytes 3145736 | tf_op jit(solution)/shard_map/ppermute | solution.py:396
  58.5 1.9 %collective-permute-done.6.refs_6_ = bf16[2,512,128]{2,1,0:T(8,128)(2,1)S(1)} collective-permute-done((bf16[2,512,128]{2,1,0:T(8,128)(2,1)S(1)}, bf16[2,512,128]{2,1,0:T(8,128)(2,1)S(1)}, u32[]{:S(2)}, u32[]{:S(2)}) %collective-permute-start.6) | collective-permute-done | bytes 262176 | tf_op jit(solution)/shard_map/ppermute | solution.py:396
  60.4 2.5 %collective-permute-start.14 = (bf16[512,128]{1,0:T(8,128)(2,1)S(1)}, bf16[512,128]{1,0:T(8,128)(2,1)S(1)}, u32[]{:S(2)}, u32[]{:S(2)}) collective-permute-start(bf16[512,128]{1,0:T(8,128)(2,1)S(1)} %get-tuple-element.35), channel_id=1, source_target_pairs={{0,24},{4,28},{8,16},{12,20},{16,8},{20,12},{24,0},{28,4},{1,25},{... | collective-permute-start | bytes 393224 | tf_op jit(solution)/shard_map/ppermute | solution.py:396
  62.8 1.4 %plan.1 = (s32[16]{0:T(128)S(1)}, s32[16,256]{1,0:T(8,128)S(1)}) custom-call(s32[16]{0:T(128)S(1)} %copy-done, s32[16]{0:T(128)S(1)} %copy-done.1), custom_call_target="tpu_custom_call" | custom-call | tf_op jit(solution)/shard_map/plan/pallas_call | solution.py:100
  64.3 0.8 sort.1
  65.1 1.5 %shard_map.77 = (bf16[528,128]{1,0:T(8,128)(2,1)S(1)}, bf16[4352,128]{1,0:T(8,128)(2,1)S(1)}, bf16[144,4352]{1,0:T(8,128)(2,1)S(1)}) custom-call(s32[16]{0:T(128)S(1)} %copy-done, s32[16]{0:T(128)S(1)} %get-tuple-element.21.table_ref, s32[16,256]{1,0:T(8,128)S(1)} %get-tuple-element.22.bounds_ref, ...), custom_call_target="tpu_custom_call", output_to_operand_aliasing={{1}: (4, {}), {2}: (5, {})} | custom-call | tf_op jit(solution)/shard_map/pallas_call | solution.py:285
  66.6 1.5 %shard_map.78 = bf16[528,128]{1,0:T(8,128)(2,1)S(1)} custom-call(s32[16]{0:T(128)S(1)} %copy-done, s32[16]{0:T(128)S(1)} %get-tuple-element.21.table_ref, s32[16,256]{1,0:T(8,128)S(1)} %get-tuple-element.22.bounds_ref, bf16[512,128]{1,0:T(8,128)(2,1)S(1)} %collective-permute-done.q_ref, bf16[4352,128]{1,0:T(8,128)(2,1)S(1)} %get-tuple-element.31.refs_0_, ...), custom_call_target="tpu_custom_call" | custom-call | tf_op jit(solution)/shard_map/pallas_call | solution.py:285
  68.0 0.0 collective-permute-done.12.q_ref
  68.1 0.1 collective-permute-start.8
  68.1 2.5 %shard_map.79 = bf16[528,128]{1,0:T(8,128)(2,1)S(1)} custom-call(s32[16]{0:T(128)S(1)} %copy-done, s32[16]{0:T(128)S(1)} %get-tuple-element.21.table_ref, s32[16,256]{1,0:T(8,128)S(1)} %get-tuple-element.22.bounds_ref, bf16[512,128]{1,0:T(8,128)(2,1)S(1)} %collective-permute-done.12.q_ref, bf16[4352,128]{1,0:T(8,128)(2,1)S(1)} %get-tuple-element.31.refs_0_, ...), custom_call_target="tpu_custom_call" | custom-call | tf_op jit(solution)/shard_map/pallas_call | solution.py:285
  70.6 0.0 collective-permute-done.14.q_ref
  70.6 2.0 %collective-permute-start.13 = (bf16[528,128]{1,0:T(8,128)(2,1)S(1)}, bf16[528,128]{1,0:T(8,128)(2,1)S(1)}, u32[]{:S(2)}, u32[]{:S(2)}) collective-permute-start(bf16[528,128]{1,0:T(8,128)(2,1)S(1)} %shard_map.79), channel_id=1, source_target_pairs={{0,8},{4,12},{8,0},{12,4},{16,24},{20,28},{24,16},{28,20},{1,9},{5... | collective-permute-start | bytes 405512 | tf_op jit(solution)/shard_map/ppermute | solution.py:396
  72.6 1.5 %shard_map.80 = bf16[528,128]{1,0:T(8,128)(2,1)S(1)} custom-call(s32[16]{0:T(128)S(1)} %copy-done, s32[16]{0:T(128)S(1)} %get-tuple-element.21.table_ref, s32[16,256]{1,0:T(8,128)S(1)} %get-tuple-element.22.bounds_ref, bf16[512,128]{1,0:T(8,128)(2,1)S(1)} %collective-permute-done.14.q_ref, bf16[4352,128]{1,0:T(8,128)(2,1)S(1)} %get-tuple-element.31.refs_0_, ...), custom_call_target="tpu_custom_call" | custom-call | tf_op jit(solution)/shard_map/pallas_call | solution.py:285
  74.0 0.0 collective-permute-done.18.refs_15_.refs_10_
  74.0 1.5 %collective-permute-start.15 = (bf16[528,128]{1,0:T(8,128)(2,1)S(1)}, bf16[528,128]{1,0:T(8,128)(2,1)S(1)}, u32[]{:S(2)}, u32[]{:S(2)}) collective-permute-start(bf16[528,128]{1,0:T(8,128)(2,1)S(1)} %shard_map.80), channel_id=1, source_target_pairs={{0,24},{4,28},{8,16},{12,20},{16,8},{20,12},{24,0},{28,4},{1,25},{... | collective-permute-start | bytes 405512 | tf_op jit(solution)/shard_map/ppermute | solution.py:396
  75.6 1.2 %collective-permute-done.8.refs_0_ = bf16[528,128]{1,0:T(8,128)(2,1)S(1)} collective-permute-done((bf16[528,128]{1,0:T(8,128)(2,1)S(1)}, bf16[528,128]{1,0:T(8,128)(2,1)S(1)}, u32[]{:S(2)}, u32[]{:S(2)}) %collective-permute-start.8) | collective-permute-done | bytes 135200 | tf_op jit(solution)/shard_map/ppermute | solution.py:396
  76.8 1.5 %collective-permute-start.21 = (bf16[528,128]{1,0:T(8,128)(2,1)S(1)}, bf16[528,128]{1,0:T(8,128)(2,1)S(1)}, u32[]{:S(2)}, u32[]{:S(2)}) collective-permute-start(bf16[528,128]{1,0:T(8,128)(2,1)S(1)} %get-tuple-element.33.refs_0_.refs_4_), channel_id=1, source_target_pairs={{0,2},{1,3},{2,0},{3,1},{4,6},{5,7},{6,4},{7,5},{8,10},{9,11},{10,... | collective-permute-start | bytes 405512 | tf_op jit(solution)/shard_map/ppermute | solution.py:396
  78.3 0.0 collective-permute-done.13.refs_4_.refs_5_
  78.3 0.0 collective-permute-start.20
  78.3 2.7 %collective-permute-done.15.refs_8_.refs_6_ = bf16[528,128]{1,0:T(8,128)(2,1)S(1)} collective-permute-done((bf16[528,128]{1,0:T(8,128)(2,1)S(1)}, bf16[528,128]{1,0:T(8,128)(2,1)S(1)}, u32[]{:S(2)}, u32[]{:S(2)}) %collective-permute-start.15) | collective-permute-done | bytes 135200 | tf_op jit(solution)/shard_map/ppermute | solution.py:396
  81.0 1.5 %collective-permute-start.10 = (bf16[528,128]{1,0:T(8,128)(2,1)S(1)}, bf16[528,128]{1,0:T(8,128)(2,1)S(1)}, u32[]{:S(2)}, u32[]{:S(2)}) collective-permute-start(bf16[528,128]{1,0:T(8,128)(2,1)S(1)} %collective-permute-done.8.refs_0_), channel_id=1, source_target_pairs={{0,2},{1,3},{2,0},{3,1},{4,6},{5,7},{6,4},{7,5},{8,10},{9,11},{10,... | collective-permute-start | bytes 405512 | tf_op jit(solution)/shard_map/ppermute | solution.py:396
  82.5 0.0 collective-permute-done.21.refs_2_
  82.5 1.7 %collective-permute-start.24 = (bf16[528,128]{1,0:T(8,128)(2,1)S(1)}, bf16[528,128]{1,0:T(8,128)(2,1)S(1)}, u32[]{:S(2)}, u32[]{:S(2)}) collective-permute-start(bf16[528,128]{1,0:T(8,128)(2,1)S(1)} %collective-permute-done.13.refs_4_.refs_5_), channel_id=1, source_target_pairs={{0,2},{1,3},{2,0},{3,1},{4,6},{5,7},{6,4},{7,5},{8,10},{9,11},{10,... | collective-permute-start | bytes 405512 | tf_op jit(solution)/shard_map/ppermute | solution.py:396
  84.2 1.9 %collective-permute-done.10.refs_2_ = bf16[528,128]{1,0:T(8,128)(2,1)S(1)} collective-permute-done((bf16[528,128]{1,0:T(8,128)(2,1)S(1)}, bf16[528,128]{1,0:T(8,128)(2,1)S(1)}, u32[]{:S(2)}, u32[]{:S(2)}) %collective-permute-start.10) | collective-permute-done | bytes 135200 | tf_op jit(solution)/shard_map/ppermute | solution.py:396
  86.1 1.5 %collective-permute-start.27 = (bf16[528,128]{1,0:T(8,128)(2,1)S(1)}, bf16[528,128]{1,0:T(8,128)(2,1)S(1)}, u32[]{:S(2)}, u32[]{:S(2)}) collective-permute-start(bf16[528,128]{1,0:T(8,128)(2,1)S(1)} %collective-permute-done.15.refs_8_.refs_6_), channel_id=1, source_target_pairs={{0,2},{1,3},{2,0},{3,1},{4,6},{5,7},{6,4},{7,5},{8,10},{9,11},{10,... | collective-permute-start | bytes 405512 | tf_op jit(solution)/shard_map/ppermute | solution.py:396
  87.6 0.4 collective-permute-done.24.refs_6_
  88.1 4.2 %collective-permute-start.19 = (bf16[256,1024]{1,0:T(8,128)(2,1)S(1)}, bf16[256,1024]{1,0:T(8,128)(2,1)S(1)}, u32[]{:S(2)}, u32[]{:S(2)}) collective-permute-start(bf16[256,1024]{1,0:T(8,128)(2,1)S(1)} %collective-permute-done.18.refs_15_.refs_10_), channel_id=1, source_target_pairs={{0,4},{4,0},{8,12},{12,8},{16,20},{20,16},{24,28},{28,24},{1,5},{5... | collective-permute-start | bytes 1572872 | tf_op jit(solution)/shard_map/ppermute | solution.py:396
  92.3 0.0 collective-permute-done.23.refs_5_
  92.3 0.0 collective-permute-start.26
  92.3 0.5 collective-permute-start.22
  92.8 0.8 collective-permute-done.26.refs_9_
  93.7 0.1 collective-permute-start.25
  93.8 0.0 collective-permute-done.22.refs_3_
  93.9 0.3 collective-permute-start.28
  94.2 0.8 collective-permute-done.25.refs_7_
  95.0 0.1 collective-permute-start.9
  95.2 0.0 collective-permute-done.28.refs_11_
  95.2 0.3 collective-permute-start.11
  95.5 5.6 %collective-permute-done.19.refs_16_.refs_11_ = bf16[256,1024]{1,0:T(8,128)(2,1)S(1)} collective-permute-done((bf16[256,1024]{1,0:T(8,128)(2,1)S(1)}, bf16[256,1024]{1,0:T(8,128)(2,1)S(1)}, u32[]{:S(2)}, u32[]{:S(2)}) %collective-permute-start.19) | collective-permute-done | bytes 524320 | tf_op jit(solution)/shard_map/ppermute | solution.py:396
  101.2 0.0 collective-permute-done.16.refs_13_.refs_8_
  101.2 0.0 collective-permute-done.17.refs_14_.refs_9_
  101.2 1.8 %early.1.refs_12_ = f32[512,1024]{1,0:T(8,128)S(1)} custom-call(bf16[528,128]{1,0:T(8,128)(2,1)S(1)} %get-tuple-element.33.refs_0_.refs_4_, bf16[528,128]{1,0:T(8,128)(2,1)S(1)} %collective-permute-done.20.refs_1_, bf16[528,128]{1,0:T(8,128)(2,1)S(1)} %collective-permute-done.21.refs_2_, bf16[528,128]{1,0:T(8,128)(2,1)S(1)} %collective-permute-done.22.refs_3_, ...), custom_call_target="tpu_custom_call" | custom-call | tf_op jit(solution)/shard_map/early/pallas_call | solution.py:367
  103.0 0.0 collective-permute-done.9.refs_1_
  103.0 1.7 %late.1 = (bf16[512,1024]{1,0:T(8,128)(2,1)}, f32[4,512]{1,0:T(4,128)}) custom-call(bf16[528,128]{1,0:T(8,128)(2,1)S(1)} %collective-permute-done.8.refs_0_, bf16[528,128]{1,0:T(8,128)(2,1)S(1)} %collective-permute-done.9.refs_1_, bf16[528,128]{1,0:T(8,128)(2,1)S(1)} %collective-permute-done.10.refs_2_, ...), custom_call_target="tpu_custom_call" | custom-call | tf_op jit(solution)/shard_map/late/pallas_call | solution.py:376
  (8 shorter events, 0.0 us)
Async XLA Ops:
  2.3 35.8 %collective-permute-start.2 = (bf16[2,512,128]{2,1,0:T(8,128)(2,1)S(1)}, bf16[2,512,128]{2,1,0:T(8,128)(2,1)S(1)}, u32[]{:S(2)}, u32[]{:S(2)}) collective-permute-start(bf16[2,512,128]{2,1,0:T(8,128)(2,1)S(1)} %get-tuple-element.26), channel_id=1, source_target_pairs={{0,8},{4,12},{8,0},{12,4},{16,24},{20,28},{24,16},{28,20},{1,9},{5... | collective-permute-start | bytes 786440 | tf_op jit(solution)/shard_map/ppermute | solution.py:396
  5.4 33.2 %collective-permute-start.4 = (bf16[2,512,128]{2,1,0:T(8,128)(2,1)S(1)}, bf16[2,512,128]{2,1,0:T(8,128)(2,1)S(1)}, u32[]{:S(2)}, u32[]{:S(2)}) collective-permute-start(bf16[2,512,128]{2,1,0:T(8,128)(2,1)S(1)} %get-tuple-element.27), channel_id=1, source_target_pairs={{0,16},{4,20},{8,24},{12,28},{16,0},{20,4},{24,8},{28,12},{1,17},{... | collective-permute-start | bytes 786440 | tf_op jit(solution)/shard_map/ppermute | solution.py:396
  8.0 32.1 %collective-permute-start.5 = (bf16[2,512,128]{2,1,0:T(8,128)(2,1)S(1)}, bf16[2,512,128]{2,1,0:T(8,128)(2,1)S(1)}, u32[]{:S(2)}, u32[]{:S(2)}) collective-permute-start(bf16[2,512,128]{2,1,0:T(8,128)(2,1)S(1)} %get-tuple-element.28), channel_id=1, source_target_pairs={{0,24},{4,28},{8,16},{12,20},{16,8},{20,12},{24,0},{28,4},{1,25},{... | collective-permute-start | bytes 786440 | tf_op jit(solution)/shard_map/ppermute | solution.py:396
  8.0 54.9 %copy-start = (s32[16]{0:T(128)S(1)}, s32[16]{0:T(128)}, u32[]{:S(2)}) copy-start(s32[16]{0:T(128)} %layout_ref.11) | copy-start | bytes 196
  8.0 54.9 %copy-start.1 = (s32[16]{0:T(128)S(1)}, s32[16]{0:T(128)}, u32[]{:S(2)}) copy-start(s32[16]{0:T(128)} %lens_ref.1) | copy-start | bytes 196
  8.0 28.6 %collective-permute-start = (bf16[512,128]{1,0:T(8,128)(2,1)S(1)}, bf16[512,128]{1,0:T(8,128)(2,1)S(1)}, u32[]{:S(2)}, u32[]{:S(2)}) collective-permute-start(bf16[512,128]{1,0:T(8,128)(2,1)S(1)} %get-tuple-element.23), channel_id=1, source_target_pairs={{0,16},{4,20},{8,24},{12,28},{16,0},{20,4},{24,8},{28,12},{1,17},{... | collective-permute-start | bytes 393224 | tf_op jit(solution)/shard_map/ppermute | solution.py:396
  11.9 62.1 %collective-permute-start.18 = (bf16[256,1024]{1,0:T(8,128)(2,1)S(1)}, bf16[256,1024]{1,0:T(8,128)(2,1)S(1)}, u32[]{:S(2)}, u32[]{:S(2)}) collective-permute-start(bf16[256,1024]{1,0:T(8,128)(2,1)S(1)} %get-tuple-element.39), channel_id=1, source_target_pairs={{0,3},{1,2},{2,1},{3,0},{4,7},{5,6},{6,5},{7,4},{8,11},{9,10},{10,... | collective-permute-start | bytes 1572872 | tf_op jit(solution)/shard_map/ppermute | solution.py:396
  36.6 9.2 %collective-permute-start.1 = (bf16[2,512,128]{2,1,0:T(8,128)(2,1)S(1)}, bf16[2,512,128]{2,1,0:T(8,128)(2,1)S(1)}, u32[]{:S(2)}, u32[]{:S(2)}) collective-permute-start(bf16[2,512,128]{2,1,0:T(8,128)(2,1)S(1)} %get-tuple-element.25.refs_0_), channel_id=1, source_target_pairs={{0,4},{4,0},{8,12},{12,8},{16,20},{20,16},{24,28},{28,24},{1,5},{5... | collective-permute-start | bytes 786440 | tf_op jit(solution)/shard_map/ppermute | solution.py:396
  38.1 13.3 %collective-permute-start.3 = (bf16[2,512,128]{2,1,0:T(8,128)(2,1)S(1)}, bf16[2,512,128]{2,1,0:T(8,128)(2,1)S(1)}, u32[]{:S(2)}, u32[]{:S(2)}) collective-permute-start(bf16[2,512,128]{2,1,0:T(8,128)(2,1)S(1)} %collective-permute-done.2.refs_2_), channel_id=1, source_target_pairs={{0,4},{4,0},{8,12},{12,8},{16,20},{20,16},{24,28},{28,24},{1,5},{5... | collective-permute-start | bytes 786440 | tf_op jit(solution)/shard_map/ppermute | solution.py:396
  38.6 18.4 %collective-permute-start.7 = (bf16[2,512,128]{2,1,0:T(8,128)(2,1)S(1)}, bf16[2,512,128]{2,1,0:T(8,128)(2,1)S(1)}, u32[]{:S(2)}, u32[]{:S(2)}) collective-permute-start(bf16[2,512,128]{2,1,0:T(8,128)(2,1)S(1)} %collective-permute-done.4.refs_4_), channel_id=1, source_target_pairs={{0,4},{4,0},{8,12},{12,8},{16,20},{20,16},{24,28},{28,24},{1,5},{5... | collective-permute-start | bytes 786440 | tf_op jit(solution)/shard_map/ppermute | solution.py:396
  40.1 20.3 %collective-permute-start.6 = (bf16[2,512,128]{2,1,0:T(8,128)(2,1)S(1)}, bf16[2,512,128]{2,1,0:T(8,128)(2,1)S(1)}, u32[]{:S(2)}, u32[]{:S(2)}) collective-permute-start(bf16[2,512,128]{2,1,0:T(8,128)(2,1)S(1)} %collective-permute-done.5.refs_5_), channel_id=1, source_target_pairs={{0,4},{4,0},{8,12},{12,8},{16,20},{20,16},{24,28},{28,24},{1,5},{5... | collective-permute-start | bytes 786440 | tf_op jit(solution)/shard_map/ppermute | solution.py:396
  45.7 22.3 %collective-permute-start.12 = (bf16[512,128]{1,0:T(8,128)(2,1)S(1)}, bf16[512,128]{1,0:T(8,128)(2,1)S(1)}, u32[]{:S(2)}, u32[]{:S(2)}) collective-permute-start(bf16[512,128]{1,0:T(8,128)(2,1)S(1)} %get-tuple-element.34), channel_id=1, source_target_pairs={{0,8},{4,12},{8,0},{12,4},{16,24},{20,28},{24,16},{28,20},{1,9},{5... | collective-permute-start | bytes 393224 | tf_op jit(solution)/shard_map/ppermute | solution.py:396
  51.4 49.8 %collective-permute-start.16 = (bf16[512,1024]{1,0:T(8,128)(2,1)S(1)}, bf16[512,1024]{1,0:T(8,128)(2,1)S(1)}, u32[]{:S(2)}, u32[]{:S(2)}) collective-permute-start(bf16[512,1024]{1,0:T(8,128)(2,1)S(1)} %get-tuple-element.37), channel_id=1, source_target_pairs={{0,1},{1,0},{2,3},{3,2},{4,5},{5,4},{6,7},{7,6},{8,9},{9,8},{10,11... | collective-permute-start | bytes 3145736 | tf_op jit(solution)/shard_map/ppermute | solution.py:396
  57.0 44.2 %collective-permute-start.17 = (bf16[512,1024]{1,0:T(8,128)(2,1)S(1)}, bf16[512,1024]{1,0:T(8,128)(2,1)S(1)}, u32[]{:S(2)}, u32[]{:S(2)}) collective-permute-start(bf16[512,1024]{1,0:T(8,128)(2,1)S(1)} %get-tuple-element.38), channel_id=1, source_target_pairs={{0,2},{1,3},{2,0},{3,1},{4,6},{5,7},{6,4},{7,5},{8,10},{9,11},{10,... | collective-permute-start | bytes 3145736 | tf_op jit(solution)/shard_map/ppermute | solution.py:396
  60.4 10.2 %collective-permute-start.14 = (bf16[512,128]{1,0:T(8,128)(2,1)S(1)}, bf16[512,128]{1,0:T(8,128)(2,1)S(1)}, u32[]{:S(2)}, u32[]{:S(2)}) collective-permute-start(bf16[512,128]{1,0:T(8,128)(2,1)S(1)} %get-tuple-element.35), channel_id=1, source_target_pairs={{0,24},{4,28},{8,16},{12,20},{16,8},{20,12},{24,0},{28,4},{1,25},{... | collective-permute-start | bytes 393224 | tf_op jit(solution)/shard_map/ppermute | solution.py:396
  68.1 8.7 %collective-permute-start.8 = (bf16[528,128]{1,0:T(8,128)(2,1)S(1)}, bf16[528,128]{1,0:T(8,128)(2,1)S(1)}, u32[]{:S(2)}, u32[]{:S(2)}) collective-permute-start(bf16[528,128]{1,0:T(8,128)(2,1)S(1)} %shard_map.78), channel_id=1, source_target_pairs={{0,16},{4,20},{8,24},{12,28},{16,0},{20,4},{24,8},{28,12},{1,17},{... | collective-permute-start | bytes 405512 | tf_op jit(solution)/shard_map/ppermute | solution.py:396
  70.6 7.7 %collective-permute-start.13 = (bf16[528,128]{1,0:T(8,128)(2,1)S(1)}, bf16[528,128]{1,0:T(8,128)(2,1)S(1)}, u32[]{:S(2)}, u32[]{:S(2)}) collective-permute-start(bf16[528,128]{1,0:T(8,128)(2,1)S(1)} %shard_map.79), channel_id=1, source_target_pairs={{0,8},{4,12},{8,0},{12,4},{16,24},{20,28},{24,16},{28,20},{1,9},{5... | collective-permute-start | bytes 405512 | tf_op jit(solution)/shard_map/ppermute | solution.py:396
  74.0 7.0 %collective-permute-start.15 = (bf16[528,128]{1,0:T(8,128)(2,1)S(1)}, bf16[528,128]{1,0:T(8,128)(2,1)S(1)}, u32[]{:S(2)}, u32[]{:S(2)}) collective-permute-start(bf16[528,128]{1,0:T(8,128)(2,1)S(1)} %shard_map.80), channel_id=1, source_target_pairs={{0,24},{4,28},{8,16},{12,20},{16,8},{20,12},{24,0},{28,4},{1,25},{... | collective-permute-start | bytes 405512 | tf_op jit(solution)/shard_map/ppermute | solution.py:396
  76.8 5.8 %collective-permute-start.21 = (bf16[528,128]{1,0:T(8,128)(2,1)S(1)}, bf16[528,128]{1,0:T(8,128)(2,1)S(1)}, u32[]{:S(2)}, u32[]{:S(2)}) collective-permute-start(bf16[528,128]{1,0:T(8,128)(2,1)S(1)} %get-tuple-element.33.refs_0_.refs_4_), channel_id=1, source_target_pairs={{0,2},{1,3},{2,0},{3,1},{4,6},{5,7},{6,4},{7,5},{8,10},{9,11},{10,... | collective-permute-start | bytes 405512 | tf_op jit(solution)/shard_map/ppermute | solution.py:396
  78.3 5.9 %collective-permute-start.20 = (bf16[528,128]{1,0:T(8,128)(2,1)S(1)}, bf16[528,128]{1,0:T(8,128)(2,1)S(1)}, u32[]{:S(2)}, u32[]{:S(2)}) collective-permute-start(bf16[528,128]{1,0:T(8,128)(2,1)S(1)} %get-tuple-element.33.refs_0_.refs_4_), channel_id=1, source_target_pairs={{0,1},{1,0},{2,3},{3,2},{4,5},{5,4},{6,7},{7,6},{8,9},{9,8},{10,11... | collective-permute-start | bytes 405512 | tf_op jit(solution)/shard_map/ppermute | solution.py:396
  81.0 5.1 %collective-permute-start.10 = (bf16[528,128]{1,0:T(8,128)(2,1)S(1)}, bf16[528,128]{1,0:T(8,128)(2,1)S(1)}, u32[]{:S(2)}, u32[]{:S(2)}) collective-permute-start(bf16[528,128]{1,0:T(8,128)(2,1)S(1)} %collective-permute-done.8.refs_0_), channel_id=1, source_target_pairs={{0,2},{1,3},{2,0},{3,1},{4,6},{5,7},{6,4},{7,5},{8,10},{9,11},{10,... | collective-permute-start | bytes 405512 | tf_op jit(solution)/shard_map/ppermute | solution.py:396
  82.5 5.6 %collective-permute-start.24 = (bf16[528,128]{1,0:T(8,128)(2,1)S(1)}, bf16[528,128]{1,0:T(8,128)(2,1)S(1)}, u32[]{:S(2)}, u32[]{:S(2)}) collective-permute-start(bf16[528,128]{1,0:T(8,128)(2,1)S(1)} %collective-permute-done.13.refs_4_.refs_5_), channel_id=1, source_target_pairs={{0,2},{1,3},{2,0},{3,1},{4,6},{5,7},{6,4},{7,5},{8,10},{9,11},{10,... | collective-permute-start | bytes 405512 | tf_op jit(solution)/shard_map/ppermute | solution.py:396
  84.2 8.1 %collective-permute-start.23 = (bf16[528,128]{1,0:T(8,128)(2,1)S(1)}, bf16[528,128]{1,0:T(8,128)(2,1)S(1)}, u32[]{:S(2)}, u32[]{:S(2)}) collective-permute-start(bf16[528,128]{1,0:T(8,128)(2,1)S(1)} %collective-permute-done.13.refs_4_.refs_5_), channel_id=1, source_target_pairs={{0,1},{1,0},{2,3},{3,2},{4,5},{5,4},{6,7},{7,6},{8,9},{9,8},{10,11... | collective-permute-start | bytes 405512 | tf_op jit(solution)/shard_map/ppermute | solution.py:396
  86.1 6.2 %collective-permute-start.27 = (bf16[528,128]{1,0:T(8,128)(2,1)S(1)}, bf16[528,128]{1,0:T(8,128)(2,1)S(1)}, u32[]{:S(2)}, u32[]{:S(2)}) collective-permute-start(bf16[528,128]{1,0:T(8,128)(2,1)S(1)} %collective-permute-done.15.refs_8_.refs_6_), channel_id=1, source_target_pairs={{0,2},{1,3},{2,0},{3,1},{4,6},{5,7},{6,4},{7,5},{8,10},{9,11},{10,... | collective-permute-start | bytes 405512 | tf_op jit(solution)/shard_map/ppermute | solution.py:396
  88.1 13.1 %collective-permute-start.19 = (bf16[256,1024]{1,0:T(8,128)(2,1)S(1)}, bf16[256,1024]{1,0:T(8,128)(2,1)S(1)}, u32[]{:S(2)}, u32[]{:S(2)}) collective-permute-start(bf16[256,1024]{1,0:T(8,128)(2,1)S(1)} %collective-permute-done.18.refs_15_.refs_10_), channel_id=1, source_target_pairs={{0,4},{4,0},{8,12},{12,8},{16,20},{20,16},{24,28},{28,24},{1,5},{5... | collective-permute-start | bytes 1572872 | tf_op jit(solution)/shard_map/ppermute | solution.py:396
  92.3 1.4 %collective-permute-start.26 = (bf16[528,128]{1,0:T(8,128)(2,1)S(1)}, bf16[528,128]{1,0:T(8,128)(2,1)S(1)}, u32[]{:S(2)}, u32[]{:S(2)}) collective-permute-start(bf16[528,128]{1,0:T(8,128)(2,1)S(1)} %collective-permute-done.15.refs_8_.refs_6_), channel_id=1, source_target_pairs={{0,1},{1,0},{2,3},{3,2},{4,5},{5,4},{6,7},{7,6},{8,9},{9,8},{10,11... | collective-permute-start | bytes 405512 | tf_op jit(solution)/shard_map/ppermute | solution.py:396
  92.3 1.5 %collective-permute-start.22 = (bf16[528,128]{1,0:T(8,128)(2,1)S(1)}, bf16[528,128]{1,0:T(8,128)(2,1)S(1)}, u32[]{:S(2)}, u32[]{:S(2)}) collective-permute-start(bf16[528,128]{1,0:T(8,128)(2,1)S(1)} %collective-permute-done.21.refs_2_), channel_id=1, source_target_pairs={{0,1},{1,0},{2,3},{3,2},{4,5},{5,4},{6,7},{7,6},{8,9},{9,8},{10,11... | collective-permute-start | bytes 405512 | tf_op jit(solution)/shard_map/ppermute | solution.py:396
  93.7 1.4 %collective-permute-start.25 = (bf16[528,128]{1,0:T(8,128)(2,1)S(1)}, bf16[528,128]{1,0:T(8,128)(2,1)S(1)}, u32[]{:S(2)}, u32[]{:S(2)}) collective-permute-start(bf16[528,128]{1,0:T(8,128)(2,1)S(1)} %collective-permute-done.24.refs_6_), channel_id=1, source_target_pairs={{0,1},{1,0},{2,3},{3,2},{4,5},{5,4},{6,7},{7,6},{8,9},{9,8},{10,11... | collective-permute-start | bytes 405512 | tf_op jit(solution)/shard_map/ppermute | solution.py:396
  93.9 1.4 %collective-permute-start.28 = (bf16[528,128]{1,0:T(8,128)(2,1)S(1)}, bf16[528,128]{1,0:T(8,128)(2,1)S(1)}, u32[]{:S(2)}, u32[]{:S(2)}) collective-permute-start(bf16[528,128]{1,0:T(8,128)(2,1)S(1)} %collective-permute-done.27.refs_10_), channel_id=1, source_target_pairs={{0,1},{1,0},{2,3},{3,2},{4,5},{5,4},{6,7},{7,6},{8,9},{9,8},{10,11... | collective-permute-start | bytes 405512 | tf_op jit(solution)/shard_map/ppermute | solution.py:396
  95.0 8.0 %collective-permute-start.9 = (bf16[528,128]{1,0:T(8,128)(2,1)S(1)}, bf16[528,128]{1,0:T(8,128)(2,1)S(1)}, u32[]{:S(2)}, u32[]{:S(2)}) collective-permute-start(bf16[528,128]{1,0:T(8,128)(2,1)S(1)} %collective-permute-done.8.refs_0_), channel_id=1, source_target_pairs={{0,1},{1,0},{2,3},{3,2},{4,5},{5,4},{6,7},{7,6},{8,9},{9,8},{10,11... | collective-permute-start | bytes 405512 | tf_op jit(solution)/shard_map/ppermute | solution.py:396
  95.2 7.8 %collective-permute-start.11 = (bf16[528,128]{1,0:T(8,128)(2,1)S(1)}, bf16[528,128]{1,0:T(8,128)(2,1)S(1)}, u32[]{:S(2)}, u32[]{:S(2)}) collective-permute-start(bf16[528,128]{1,0:T(8,128)(2,1)S(1)} %collective-permute-done.10.refs_2_), channel_id=1, source_target_pairs={{0,1},{1,0},{2,3},{3,2},{4,5},{5,4},{6,7},{7,6},{8,9},{9,8},{10,11... | collective-permute-start | bytes 405512 | tf_op jit(solution)/shard_map/ppermute | solution.py:396
